TPU v7x, 32 devices: a whole 2x2x4 slice. The times are simulated.
32 devices in a mesh: seq: 8 (over z, x), head: 4 (over y, core).
Axes of the slice: x: 2, y: 2, z: 4, core: 2. Of those that a mesh axis runs over, the one named last changes fastest.
Arguments:
- queries: bfloat16 [8192, 4096], P('seq', 'head'), may hold values from -150 to 150
- keys: bfloat16 [8192, 4096], P('seq', 'head'), may hold values from -7 to 7
- values: bfloat16 [8192, 4096], P('seq', 'head'), may hold values from -6 to 6
- random_holder: int32 [32, 64, 3], P('head', 'seq'), may hold values from 0 to 7, all different within a row; in each aligned block of 8 rows (0 to 7, 8 to 15, ..., all dimensions but the last counted through in order) at most 3 rows name the same one
- random_offset: int32 [32, 64, 3], P('head', 'seq'), may hold values from 0 to 7
- keep: int32 [64], P('seq'), may hold values from 0 to 1, as said below
Outputs:
- packed: bfloat16 [8192, 4096], P('seq', 'head')
Inputs may be any that keep to these rules, and one draw needn't show every extreme that they name: `random_holder`: for each head, the 8 query blocks of one index of seq name no index of seq more than 3 times over all their random entries; the 3 entries of one query block and head differ. `keep`: block j is kept where j % 8 == 0 or j % 8 == 7, and not kept where j % 8 == 1.
All inputs are finite; a program needn't handle non-finite values.
Results may differ from a plain program's by a relative error of at most 0.007.
Values may be sent and summed in bfloat16 or wider, within the bound.
No kernel may reach another device: no remote copies, remote signals or barrier semaphores. Data moves between devices by JAX's collectives and lax.ppermute only.
A program may use at most 128 MiB of HBM per device.

v0:
```python
import functools
import math

import jax
import jax.numpy as jnp
from jax import lax
from jax.experimental import pallas as pl
from jax.experimental.pallas import tpu as pltpu
from jax.sharding import PartitionSpec as P

DH = 128
B = 128
G = 2
R = 3
LANES = 128

neg_big = -1e30

ROUTE_SHARES = ((0.66, 0.545, 0.61), (0.73, 0.6, 0.7), (1.0, 1.0, 1.0))
PACK_SHARES = ((0.7, 0.35, 0.75), (0.8, 0.45, 0.85), (1.0, 1.0, 1.0))
PARTS = 2
SPLIT = (4, 6)


def log2(size):
    assert size & (size - 1) == 0
    return size.bit_length() - 1


class Plan:
    def __init__(self, count, groups, blk_dev, head_dev):
        self.count, self.groups, self.blk, self.heads = count, groups, blk_dev, head_dev
        self.bits = log2(count)
        self.stride = groups * head_dev
        self.lanes = count * self.stride
        self.blocks = count * blk_dev
        self.req = blk_dev * R
        self.per_head = blk_dev + 2 + G
        self.own = blk_dev * head_dev
        most = max(2, (self.req + count - 1) // count)
        bound = (count // 2) * most * head_dev
        self.full = [min(self.own << s, bound) for s in range(self.bits)]
        self.base = [sum(self.full[:s]) for s in range(self.bits)]
        self.pool = head_dev * self.per_head + sum(self.full)
        self.cfull = [
            min((blk_dev - 1) << s, blk_dev << (self.bits - 1 - s)) for s in range(self.bits)
        ]
        self.cbase = [sum(self.cfull[:s]) for s in range(self.bits)]
        self.width = -(-max(self.full + self.cfull) // LANES) * LANES

    def sizes(self, full, shares):
        out = []
        for s in range(self.bits):
            share = shares[0] if s == 0 else shares[2] if s == self.bits - 1 else shares[1]
            out.append(min(full[s], max(1, math.ceil(full[s] * share))))
        return out

    def route_sizes(self):
        return [self.sizes(self.full, shares) for shares in ROUTE_SHARES]

    def pack_sizes(self):
        return [self.sizes(self.cfull, shares) for shares in PACK_SHARES]

    def rows(self):
        return 2 * self.bits + 4


def iota(shape, axis):
    return lax.broadcasted_iota(jnp.int32, shape, axis)


def flag(cond):
    return jnp.where(cond, 1.0, 0.0)


def dot(a, b):
    return jnp.dot(
        a.astype(jnp.bfloat16), b.astype(jnp.bfloat16), preferred_element_type=jnp.float32
    )


def choose(tops, sizes):
    index = jnp.int32(len(sizes) - 1)
    for number in reversed(range(len(sizes) - 1)):
        fits = functools.reduce(
            jnp.logical_and, [top <= float(size) for top, size in zip(tops, sizes[number])]
        )
        index = jnp.where(fits, jnp.int32(number), index)
    return index


def lists_body(plan, scal, ids, own_ids, lists, table):
    me, group = scal[0], scal[1]
    T, L, hd = plan.blocks, plan.lanes, plan.heads
    lb, ls, lh = log2(plan.blk), log2(plan.stride), log2(hd)
    W = plan.width
    t = iota((T, L), 0)
    lane = iota((T, L), 1)
    holder = jnp.right_shift(lane, ls)
    need = jnp.zeros((T, L), jnp.int32)
    for k in range(plan.req):
        need = jnp.where(t == ids[k : k + 1, :], 1, need)
    near = (t >= holder * plan.blk - 1) & (t <= (holder + 1) * plan.blk)
    need = jnp.where(near | (t < G), 0, need)
    needb = need.astype(jnp.float32).astype(jnp.bfloat16)
    x = iota((L, L), 0)
    y = iota((L, L), 1)
    lower = flag(iota((T, T), 0) > iota((T, T), 1)).astype(jnp.bfloat16)
    upper = flag(iota((hd, hd), 0) < iota((hd, hd), 1)).astype(jnp.bfloat16)
    same = flag(jnp.right_shift(x, lh) == jnp.right_shift(y, lh)).astype(jnp.bfloat16)
    xe = iota((L, hd), 0)
    he = iota((L, hd), 1)
    th = iota((T, hd), 0)
    hh = iota((T, hd), 1)
    blk_of = jnp.right_shift(th, lb)
    pos_of = th & (plan.blk - 1)
    is_own = blk_of == me
    loc = jnp.where(is_own, jnp.left_shift(hh, lb) + pos_of, 0)
    slot_w = iota((T, W), 1)
    tops = []

    def order(mask):
        within = jnp.dot(lower, mask.astype(jnp.bfloat16), preferred_element_type=jnp.float32)
        cols = jnp.broadcast_to(jnp.sum(mask, axis=0, keepdims=True), (8, hd))
        return within + dot(cols, upper)[0:1, :]

    for s in range(plan.bits):
        b = plan.bits - 1 - s
        free = ((1 << b) - 1) << ls
        group_of = flag(((x ^ y) & ~free) == 0).astype(jnp.bfloat16)
        wanted = jnp.dot(needb, group_of, preferred_element_type=jnp.float32)
        into = ((jnp.right_shift(t, lb) ^ holder ^ (1 << b)) & ((2 << b) - 1)) == 0
        recv = flag((wanted > 0.5) & into)
        cols = jnp.broadcast_to(jnp.sum(recv, axis=0, keepdims=True), (8, L))
        tops.append(jnp.max(dot(cols, same)))
        recvb = recv.astype(jnp.bfloat16)
        mine = flag(xe == me * plan.stride + group * hd + he).astype(jnp.bfloat16)
        theirs = flag(xe == (me ^ (1 << b)) * plan.stride + group * hd + he).astype(jnp.bfloat16)
        got = jnp.dot(recvb, mine, preferred_element_type=jnp.float32)
        sent = jnp.dot(recvb, theirs, preferred_element_type=jnp.float32)
        place = jnp.where(sent > 0.5, order(sent).astype(jnp.int32), -1)
        line = jnp.zeros((1, W), jnp.int32)
        for h in range(hd):
            hit = place[:, h : h + 1] == slot_w
            line = line + jnp.sum(
                jnp.where(hit, loc[:, h : h + 1] + 1, 0), axis=0, keepdims=True
            )
        lists[s : s + 1, :] = line
        loc = jnp.where(
            got > 0.5, plan.own + plan.base[s] + order(got).astype(jnp.int32), loc
        )
    per = plan.per_head
    at = jnp.where(is_own, hh * per + 1 + pos_of, loc + hd * (per - plan.blk))
    at = jnp.where(th == me * plan.blk - 1, hh * per, at)
    at = jnp.where(th == (me + 1) * plan.blk, hh * per + 1 + plan.blk, at)
    at = jnp.where((th < G) & ~is_own, hh * per + 2 + plan.blk + th, at)
    for k in range(plan.req):
        hit = th == own_ids[k : k + 1, :]
        table[k : k + 1, 0:hd] = jnp.sum(jnp.where(hit, at, 0), axis=0, keepdims=True)

    kept = jnp.zeros((T, L), jnp.int32)
    head_lane = (jnp.right_shift(t, lb) == holder) & ((lane & (plan.stride - 1)) == 0)
    for i in range(plan.blk):
        hit = head_lane & ((t & (plan.blk - 1)) == i)
        kept = kept + jnp.where(hit, ids[plan.req + i : plan.req + i + 1, :], 0)
    kept = jnp.broadcast_to(jnp.sum(kept, axis=1, keepdims=True), (T, W))
    tw = iota((T, W), 0)
    dev = jnp.right_shift(tw, lb)

    def before(mask):
        return jnp.dot(
            lower, mask.astype(jnp.float32).astype(jnp.bfloat16), preferred_element_type=jnp.float32
        ).astype(jnp.int32)

    rank = before(kept)
    dest = jnp.right_shift(rank, lb)
    cloc = jnp.where(dev == me, tw & (plan.blk - 1), 0)
    ctops = []
    for s in range(plan.bits):
        b = plan.bits - 1 - s
        ok = (kept > 0) & (jnp.right_shift(dest ^ slot_w, b) == 0)
        ok = ok & (((dev ^ slot_w ^ (1 << b)) & ((2 << b) - 1)) == 0)
        recv = jnp.where(ok, 1, 0)
        ctops.append(jnp.max(jnp.sum(recv.astype(jnp.float32), axis=0, keepdims=True)))
        got = jnp.sum(jnp.where(slot_w == me, recv, 0), axis=1, keepdims=True)
        sent = jnp.sum(jnp.where(slot_w == (me ^ (1 << b)), recv, 0), axis=1, keepdims=True)
        got = jnp.broadcast_to(got, (T, W))
        sent = jnp.broadcast_to(sent, (T, W))
        hit = (sent > 0) & (before(sent) == slot_w)
        row = plan.bits + s
        lists[row : row + 1, :] = jnp.sum(jnp.where(hit, cloc + 1, 0), axis=0, keepdims=True)
        cloc = jnp.where(got > 0, plan.blk + plan.cbase[s] + before(got), cloc)
    row = 2 * plan.bits
    hit = (kept > 0) & (rank == me * plan.blk + slot_w) & (slot_w < plan.blk)
    lists[row : row + 1, :] = jnp.sum(jnp.where(hit, cloc + 1, 0), axis=0, keepdims=True)
    both = [a + c for a, c in zip(plan.route_sizes(), plan.pack_sizes())]
    lists[row + 1 : row + 2, :] = jnp.broadcast_to(choose(tops + ctops, both), (1, W))
    first = jnp.sum(jnp.where(tw < me * plan.blk, kept, 0), axis=0, keepdims=True)
    hit = (kept > 0) & (dev == me) & (rank - first == slot_w)
    lists[row + 2 : row + 3, :] = jnp.sum(
        jnp.where(hit, tw & (plan.blk - 1), 0), axis=0, keepdims=True
    )
    lists[row + 3 : row + 4, :] = jnp.sum(
        jnp.where((dev == me), kept, 0), axis=0, keepdims=True
    )


SMEM = pl.BlockSpec(memory_space=pltpu.SMEM)
VMEM = pl.BlockSpec(memory_space=pltpu.VMEM)
HBM = pl.BlockSpec(memory_space=pltpu.HBM)
ANY = pl.BlockSpec(memory_space=pl.ANY)


def make_lists(plan, scal, ids, own_ids):
    return pl.pallas_call(
        functools.partial(lists_body, plan),
        out_shape=(
            jax.ShapeDtypeStruct((plan.rows(), plan.width), jnp.int32),
            jax.ShapeDtypeStruct((plan.req, LANES), jnp.int32),
        ),
        in_specs=[SMEM, VMEM, VMEM],
        out_specs=(VMEM, VMEM),
        name="make_lists",
    )(scal, ids, own_ids)


def pack_body(row, size, bases, own_part, rows, lists, *refs):
    sources, out = refs[1:-1], refs[-1]

    def step(j, carry):
        code = jnp.maximum(lists[row, j] - 1, 0)
        target = pl.ds(pl.multiple_of(j * rows, rows), rows)

        @pl.when(code < bases[0])
        def _():
            out[target, :] = own_part(sources[0], code)

        for number, source in enumerate(sources[1:]):
            low = bases[number]

            @pl.when((code >= low) & (code < bases[number + 1]))
            def _():
                at = pl.multiple_of((code - low) * rows, rows)
                out[target, :] = source[pl.ds(at, rows), :]

        return carry

    lax.fori_loop(0, size, step, 0)


def pack(row, size, bases, own_part, rows, lists, after, sources, width, name):
    return pl.pallas_call(
        functools.partial(pack_body, row, size, bases, own_part, rows),
        out_shape=jax.ShapeDtypeStruct((size * rows, width), jnp.bfloat16),
        in_specs=[SMEM, ANY] + [VMEM] * len(sources),
        out_specs=VMEM,
        name=name,
    )(lists, after, *sources)


def either_body(after, scal, a, b, out):
    @pl.when(scal[2] == 0)
    def _():
        out[...] = a[...]

    @pl.when(scal[2] != 0)
    def _():
        out[...] = b[...]


def either(after, cond, a, b):
    return pl.pallas_call(
        either_body,
        out_shape=jax.ShapeDtypeStruct(a.shape, a.dtype),
        in_specs=[ANY, SMEM, VMEM, VMEM],
        out_specs=VMEM,
        name="either",
    )(after, cond, a, b)


def edges_body(after, keys, values, low, high, first_keys, first_values):
    tokens, width = keys.shape
    low[:, :width] = keys[tokens - B : tokens, :]
    low[:, width:] = values[tokens - B : tokens, :]
    high[:, :width] = keys[:B, :]
    high[:, width:] = values[:B, :]
    first_keys[...] = keys[: G * B, :]
    first_values[...] = values[: G * B, :]


def edges(after, keys, values):
    width, dtype = keys.shape[1], keys.dtype
    block = jax.ShapeDtypeStruct((B, 2 * width), dtype)
    shared = jax.ShapeDtypeStruct((G * B, width), dtype)
    return pl.pallas_call(
        edges_body,
        out_shape=(block, block, shared, shared),
        in_specs=[ANY, VMEM, VMEM],
        out_specs=(VMEM,) * 4,
        name="edges",
    )(after, keys, values)


def hold_body(after, before, x, out):
    pass


def hold(after, before, x):
    return pl.pallas_call(
        hold_body,
        out_shape=jax.ShapeDtypeStruct(x.shape, x.dtype),
        in_specs=[ANY, ANY, ANY],
        out_specs=ANY,
        input_output_aliases={2: 0},
        name="hold",
    )(after, before, x)


def tile_part(heads_bits, part, rows):
    def read(own, code):
        head = jnp.right_shift(code, heads_bits)
        pos = code & ((1 << heads_bits) - 1)
        at = pl.multiple_of(pos * B + part * rows, rows)
        return own[pl.ds(at, rows), pl.ds(pl.multiple_of(head * DH, DH), DH)]

    return read


def block_part(own, code):
    return own[pl.ds(pl.multiple_of(code * B, B), B), :]


def final_body(row, slots, bases, widths, lists, *refs):
    out = refs[-1]
    per = (len(refs) - 1) // len(widths)

    def step(j, carry):
        code = lists[row, j]
        target = pl.ds(pl.multiple_of(j * B, B), B)

        @pl.when(code == 0)
        def _():
            out[target, :] = jnp.zeros((B, out.shape[1]), out.dtype)

        for number in range(per):
            low = 0 if number == 0 else bases[number - 1]

            @pl.when((code - 1 >= low) & (code - 1 < bases[number]))
            def _():
                at = pl.multiple_of((code - 1 - low) * B, B)
                for part, width in enumerate(widths):
                    first = sum(widths[:part])
                    out[target, first : first + width] = refs[part * per + number][
                        pl.ds(at, B), :
                    ]

        return carry

    lax.fori_loop(0, slots, step, 0)


def final(row, slots, bases, lists, sources, widths):
    return pl.pallas_call(
        functools.partial(final_body, row, slots, bases, widths),
        out_shape=jax.ShapeDtypeStruct((slots * B, sum(widths)), jnp.bfloat16),
        in_specs=[SMEM] + [VMEM] * len(sources),
        out_specs=VMEM,
        name="place_blocks",
    )(lists, *sources)


FACTOR = math.log2(math.e) / math.sqrt(DH)


def scores_of(qt, kt):
    return lax.dot_general(
        qt, kt, (((1,), (1,)), ((), ())), preferred_element_type=jnp.float32
    )


def gather_parts(scores, values, top):
    total = 0.0
    acc = 0.0
    for s, vt in zip(scores, values):
        p = jnp.exp2((s - top) * FACTOR)
        total = total + jnp.sum(p, axis=1, keepdims=True)
        acc = acc + jnp.dot(p.astype(jnp.bfloat16), vt, preferred_element_type=jnp.float32)
    return total, acc


def peak(scores):
    return functools.reduce(jnp.maximum, [jnp.max(s, axis=1, keepdims=True) for s in scores])


def start_near(plan, heads, own, low, high, shared, first, pool, sem, copies):
    wide = plan.heads * DH
    for h in heads:
        cols = pl.ds(h * DH, DH)
        there = pl.ds(first * wide + h * DH, DH)
        for source, at, tiles in (
            (low.at[:, there], 0, 1),
            (own.at[:, cols], 1, plan.blk),
            (high.at[:, there], 1 + plan.blk, 1),
            (shared.at[:, cols], 2 + plan.blk, G),
        ):
            copy = pltpu.make_async_copy(
                source,
                pool.at[pl.ds((h * plan.per_head + at) * B, tiles * B), :],
                sem.at[len(copies)],
            )
            copy.start()
            copies.append(copy)


def start_far(plan, sizes, chunks, pool, sem, copies):
    rows = B // PARTS
    for part in range(PARTS):
        for s in range(plan.bits):
            copy = pltpu.make_async_copy(
                chunks[part * plan.bits + s],
                pool.at[pl.ds(plan.base[s], sizes[s]), pl.ds(part * rows, rows), :],
                sem.at[len(copies)],
            )
            copy.start()
            copies.append(copy)


def tile_reader(plan, near_pool, far_pool, at):
    split = plan.heads * plan.per_head
    inside = at < split
    row = pl.multiple_of(jnp.where(inside, at, 0) * B, B)
    near = near_pool[pl.ds(row, B), :]
    far = far_pool[jnp.where(inside, 0, at - split)]
    return jnp.where(inside, near, far)


def put_stats(stat, rows, hd, h, top, total):
    lane = lax.broadcasted_iota(jnp.int32, (B, LANES), 1)
    old = stat[rows, :]
    stat[rows, :] = jnp.where(lane == h, top, jnp.where(lane == hd + h, total, old))


def near_body(plan, lists, scal, after, q, *refs):
    k, v, low, high, shared_k, shared_v, acc_out, stat_out, kp, vp, sem = refs
    blk, hd, per = plan.blk, plan.heads, plan.per_head
    copies = []
    start_near(plan, range(hd), k, low, high, shared_k, 0, kp, sem, copies)
    start_near(plan, range(hd), v, low, high, shared_v, 1, vp, sem, copies)
    for copy in copies:
        copy.wait()
    me = scal[0]
    row = 2 * plan.bits
    win = 3 * B

    def step(kk, carry):
        i = lists[row + 2, kk]
        first = (me * blk + i) == 0
        last = (me * blk + i) == plan.blocks - 1
        col = lax.broadcasted_iota(jnp.int32, (B, win), 1)
        dead = (first & (col < B)) | (last & (col >= 2 * B))
        rows = pl.ds(pl.multiple_of(i * B, B), B)
        for h in range(hd):
            qt = q[rows, h * DH : (h + 1) * DH]
            spans = (
                pl.ds(pl.multiple_of((h * per + i) * B, B), win),
                pl.ds((h * per + 2 + blk) * B, G * B),
            )
            scores = [scores_of(qt, kp[span, :]) for span in spans]
            scores[0] = jnp.where(dead, neg_big, scores[0])
            top = peak(scores)
            total, acc = gather_parts(scores, [vp[span, :] for span in spans], top)
            acc_out[rows, h * DH : (h + 1) * DH] = acc
            stat_out[rows, h : h + 1] = top
            stat_out[rows, hd + h : hd + h + 1] = total
        return carry

    lax.fori_loop(0, lists[row + 3, 0], step, 0)


def near_attend(plan, lists, scal, after, q, ins):
    pool = plan.heads * plan.per_head * B
    return pl.pallas_call(
        functools.partial(near_body, plan),
        out_shape=(
            jax.ShapeDtypeStruct(q.shape, jnp.float32),
            jax.ShapeDtypeStruct((q.shape[0], LANES), jnp.float32),
        ),
        in_specs=[SMEM, SMEM, ANY, VMEM] + [HBM] * len(ins),
        out_specs=(VMEM, VMEM),
        scratch_shapes=[
            pltpu.VMEM((pool, DH), jnp.bfloat16),
            pltpu.VMEM((pool, DH), jnp.bfloat16),
            pltpu.SemaphoreType.DMA((8 * plan.heads,)),
        ],
        name="near_attend",
    )(lists, scal, after, q, *ins)


def far_scores_body(plan, sizes, lists, table, after, q, k, low, high, shared, *refs):
    count = PARTS * plan.bits
    chunks, (p_out, stat_out), (near, far, sem) = refs[:count], refs[count : count + 2], refs[count + 2 :]
    hd = plan.heads
    copies = []
    start_far(plan, sizes, chunks, far, sem, copies)
    start_near(plan, range(hd), k, low, high, shared, 0, near, sem, copies)
    for copy in copies:
        copy.wait()
    row = 2 * plan.bits

    def step(kk, carry):
        i = lists[row + 2, kk]
        rows = pl.ds(pl.multiple_of(i * B, B), B)
        for h in range(hd):
            qt = q[rows, h * DH : (h + 1) * DH]
            scores = [
                scores_of(qt, tile_reader(plan, near, far, table[i * R + r, h])) for r in range(R)
            ]
            top = peak(scores)
            total = 0.0
            for r, s in enumerate(scores):
                p = jnp.exp2((s - top) * FACTOR)
                total = total + jnp.sum(p, axis=1, keepdims=True)
                p_out[rows, (h * R + r) * B : (h * R + r + 1) * B] = p.astype(jnp.bfloat16)
            stat_out[rows, h : h + 1] = top
            stat_out[rows, hd + h : hd + h + 1] = total
        return carry

    lax.fori_loop(0, lists[row + 3, 0], step, 0)


def pools_of(plan):
    return [
        pltpu.VMEM((plan.heads * plan.per_head * B, DH), jnp.bfloat16),
        pltpu.VMEM((sum(plan.full), B, DH), jnp.bfloat16),
        pltpu.SemaphoreType.DMA((4 * plan.heads + PARTS * plan.bits,)),
    ]


def far_scores(plan, sizes, lists, table, after, q, k, low, high, shared, chunks):
    return pl.pallas_call(
        functools.partial(far_scores_body, plan, sizes),
        out_shape=(
            jax.ShapeDtypeStruct((q.shape[0], plan.heads * R * B), jnp.bfloat16),
            jax.ShapeDtypeStruct((q.shape[0], LANES), jnp.float32),
        ),
        in_specs=[SMEM, SMEM, ANY, VMEM] + [HBM] * (4 + len(chunks)),
        out_specs=(VMEM, VMEM),
        scratch_shapes=pools_of(plan),
        name="far_scores",
    )(lists, table, after, q, k, low, high, shared, *chunks)


def far_values_body(plan, sizes, heads, lists, table, after, p, pstat, acc_in, stat, v, low, high,
                    shared, *refs):
    count = PARTS * plan.bits
    chunks, out, (near, far, sem) = refs[:count], refs[count], refs[count + 1 :]
    hd = plan.heads
    copies = []
    start_far(plan, sizes, chunks, far, sem, copies)
    start_near(plan, heads, v, low, high, shared, 1, near, sem, copies)
    for copy in copies:
        copy.wait()
    row = 2 * plan.bits

    def step(kk, carry):
        i = lists[row + 2, kk]
        rows = pl.ds(pl.multiple_of(i * B, B), B)
        for number, h in enumerate(heads):
            acc = 0.0
            for r in range(R):
                acc = acc + jnp.dot(
                    p[rows, (number * R + r) * B : (number * R + r + 1) * B],
                    tile_reader(plan, near, far, table[i * R + r, h]),
                    preferred_element_type=jnp.float32,
                )
            far_top, near_top = pstat[rows, h : h + 1], stat[rows, h : h + 1]
            top = jnp.maximum(far_top, near_top)
            a = jnp.exp2((far_top - top) * FACTOR)
            c = jnp.exp2((near_top - top) * FACTOR)
            total = a * pstat[rows, hd + h : hd + h + 1] + c * stat[rows, hd + h : hd + h + 1]
            scale = 1.0 / total
            acc = (a * scale) * acc + (c * scale) * acc_in[rows, number * DH : (number + 1) * DH]
            out[rows, number * DH : (number + 1) * DH] = acc.astype(jnp.bfloat16)
        return carry

    lax.fori_loop(0, lists[row + 3, 0], step, 0)


def far_values(plan, sizes, heads, lists, table, after, p, pstat, acc, stat, v, low, high, shared,
               chunks):
    size = len(heads)
    assert heads[0] % size == 0

    def of_team(x, width):
        return pl.BlockSpec((x.shape[0], size * width), lambda _: (0, heads[0] // size))

    return pl.pallas_call(
        functools.partial(far_values_body, plan, sizes, heads),
        out_shape=jax.ShapeDtypeStruct((p.shape[0], len(heads) * DH), jnp.bfloat16),
        grid=(1,),
        in_specs=[SMEM, SMEM, ANY, of_team(p, R * B), VMEM, of_team(acc, DH), VMEM]
        + [HBM] * (4 + len(chunks)),
        out_specs=VMEM,
        scratch_shapes=pools_of(plan),
        name="far_values",
    )(lists, table, after, p, pstat, acc, stat, v, low, high, shared, *chunks)


def swap(x, bit, count, down_only=False):
    pairs = [(i, i ^ bit) for i in range(count) if not down_only or i & bit]
    return lax.ppermute(x, "seq", pairs)


def body(queries, keys, values, random_holder, random_offset, keep):
    tok_dev, width_dev = queries.shape
    blk_dev = tok_dev // B
    head_dev = width_dev // DH
    count = lax.axis_size("seq")
    groups = lax.axis_size("head")
    plan = Plan(count, groups, blk_dev, head_dev)
    bits = plan.bits
    me = lax.axis_index("seq")
    scal = jnp.stack((me, lax.axis_index("head"))).astype(jnp.int32)

    ids = (random_holder * blk_dev + random_offset).reshape(head_dev, plan.req).T
    asked = jnp.where(jnp.repeat(keep, R)[:, None] > 0, ids, -1)
    mine = jnp.concatenate((asked, jnp.broadcast_to(keep[:, None], (blk_dev, head_dev))), axis=0)
    everyone = lax.all_to_all(
        jnp.broadcast_to(mine[None], (count * groups,) + mine.shape),
        ("seq", "head"), split_axis=0, concat_axis=0, tiled=True,
    )
    everyone = jnp.transpose(everyone, (1, 0, 2)).reshape(mine.shape[0], plan.lanes)
    lists, table = make_lists(plan, scal, everyone, ids)

    blk_bits = log2(blk_dev)
    rows = B // PARTS
    row = 2 * bits
    cuts = [0] + [cut for cut in SPLIT if cut < head_dev] + [head_dev]
    if len(cuts) == 2:
        cuts = [0, head_dev // 2, head_dev]
    teams = [range(low, high) for low, high in zip(cuts, cuts[1:])]
    flags = lambda cond: jnp.concatenate((scal, cond.astype(jnp.int32)[None]))
    odd = flags((me & 1) == 1)

    def branch(sizes, csizes):
        def run(queries, keys, values, lists, table, scal, odd):
            got = [[] for _ in range(2 * PARTS)]
            last = [lists]

            def run_after(fn, *args):
                out = fn(last[0], *args)
                last[0] = out[0] if isinstance(out, (tuple, list)) else out
                return out

            def packed_tiles(s, chunk):
                which, part = chunk // PARTS, chunk % PARTS
                bases = [plan.own + at for at in plan.base[: s + 1]]
                return run_after(
                    lambda after: pack(
                        s, sizes[s], bases, tile_part(blk_bits, part, rows), rows, lists, after,
                        [(keys, values)[which]] + got[chunk], DH, "pack_tiles",
                    )
                )

            def stage(s, chunk):
                got[chunk].append(swap(packed_tiles(s, chunk), count >> (s + 1), count))

            def tiles(which):
                return [
                    x.reshape(-1, rows, DH)
                    for part in range(PARTS)
                    for x in got[which * PARTS + part]
                ]

            def begin(chunk, packed):
                packed = run_after(lambda after: hold(after, got[chunk - 1][0], packed))
                got[chunk].append(swap(packed, count >> 1, count))

            def hop(x, pairs):
                return lax.ppermute(x, "seq", pairs)

            stage(0, 0)
            low, high, first_keys, first_values = run_after(edges, keys, values)
            low = hop(low, [(i, i + 1) for i in range(count - 1)])
            high = hop(high, [(i + 1, i) for i in range(count - 1)])
            beside = hop(first_values, [(0, 1)])
            coming = packed_tiles(0, 1)
            held = run_after(either, odd, first_keys, beside)
            spreads = []
            for s in range(bits - 1):
                bit = count >> (s + 1)
                spreads.append(
                    (bit, [(i + j, i + j + bit) for i in range(0, count, 2 * bit) for j in (0, 1)])
                )
            chunks = 2 * PARTS
            for step in range(chunks + bits - 1):
                there = None
                if step < len(spreads):
                    bit, pairs = spreads[step]
                    there = hop(held, pairs)
                elif step == len(spreads):
                    there = swap(held, 1, count)
                if step + 1 < chunks:
                    begin(step + 1, coming)
                for s in range(1, bits):
                    if 0 <= step + 1 - s < chunks:
                        stage(s, step + 1 - s)
                    if s == 1 and step + 2 < chunks:
                        coming = packed_tiles(0, step + 2)
                if step < len(spreads):
                    held = run_after(either, flags((me & bit) != 0), held, there)
                elif step == len(spreads):
                    shared_keys = run_after(either, odd, held, there)
                    shared_values = run_after(either, odd, there, held)
                if step == max(len(spreads), chunks - 2):
                    acc, stat = run_after(
                        lambda after: near_attend(
                            plan, lists, scal, after, queries,
                            [keys, values, low, high, shared_keys, shared_values],
                        )
                    )
                if step == chunks + bits - 3:
                    p, pstat = run_after(
                        lambda after: far_scores(
                            plan, sizes, lists, table, after, queries, keys, low, high,
                            shared_keys, tiles(0),
                        )
                    )

            sources = []

            def pack_stage(s, held):
                bases = [plan.blk + at for at in plan.cbase[: s + 1]]
                packed = run_after(
                    lambda after: pack(
                        bits + s, csizes[s], bases, block_part, B, lists, after, held,
                        held[0].shape[1], "pack_blocks",
                    )
                )
                held.append(swap(packed, count >> (s + 1), count, s == 0))

            for half, heads in enumerate(teams):
                attended = run_after(
                    lambda after: far_values(
                        plan, sizes, heads, lists, table, after, p, pstat, acc, stat, values,
                        low, high, shared_values, tiles(1),
                    )
                )
                sources.append([attended])
                pack_stage(0, sources[half])
            for step in range(len(teams) + bits - 2):
                for s in range(1, bits):
                    if 0 <= step + 1 - s < len(teams):
                        pack_stage(s, sources[step + 1 - s])
            bases = [plan.blk + at for at in plan.cbase + [sum(plan.cfull)]]
            widths = [len(heads) * DH for heads in teams]
            return final(row, blk_dev, bases, lists, sum(sources, []), widths)

        return run

    return lax.switch(
        lists[row + 1, 0],
        [branch(a, c) for a, c in zip(plan.route_sizes(), plan.pack_sizes())],
        queries, keys, values, lists, table, scal, odd,
    )


def solution(mesh):
    in_specs = (
        P("seq", "head"),
        P("seq", "head"),
        P("seq", "head"),
        P("head", "seq", None),
        P("head", "seq", None),
        P("seq"),
    )
    out_specs = P("seq", "head")
    return jax.shard_map(body, mesh=mesh, in_specs=in_specs, out_specs=out_specs, check_vma=False)
```

profile of v0, /device:TPU:2, one launch (start us, length us, event | category | flops | bytes accessed | tf_op | source)
XLA Modules:
  0.0 404.4 jit_solution(4544943181426135325)
XLA Ops:
  3.3 6.1 %all-to-all-start = ((s32[32,1,256]{2,1,0:T(1,128)}), s32[32,1,256]{2,1,0:T(1,128)S(1)}, u32[]{:S(2)}, u32[]{:S(2)}) async-start(s32[32,1,256]{2,1,0:T(1,128)} %reshape.174), calls=%async_computation | async-start | bytes 65536 | tf_op jit(solution)/shard_map/all_to_all | solution.py:628
  9.6 5.9 %all-to-all-done = s32[32,1,256]{2,1,0:T(1,128)S(1)} async-done(((s32[32,1,256]{2,1,0:T(1,128)}), s32[32,1,256]{2,1,0:T(1,128)S(1)}, u32[]{:S(2)}, u32[]{:S(2)}) %all-to-all-start) | async-done | bytes 32800 | tf_op jit(solution)/shard_map/all_to_all | solution.py:628
  21.4 381.6 %conditional.1 = (bf16[1024,1024]{1,0:T(8,128)(2,1)S(1)}) conditional(s32[]{:T(128)} %bitcast.47, (s32[10,128]{1,0:T(8,128)S(1)}, bf16[1024,1024]{1,0:T(8,128)(2,1)}, bf16[1024,1024]{1,0:T(8,128)(2,1)}, s32[3]{0:T(128)S(1)}, s32[]{:T(128)}, /*index=5*/s32[2]{0:T(128)S(1)}, bf16[1024,1024]{1,0:T(8,128)(2,1)}, ...), branch_computations={%region_0.1_spmd, %region_1.2_spmd, %region_2.3_spmd} | conditional | flops 12 | bytes 163841504 | solution.py:761
  33.1 11.1 %collective-permute-done.b = bf16[256,1024]{1,0:T(8,128)(2,1)S(1)} collective-permute-done((bf16[256,1024]{1,0:T(8,128)(2,1)}, bf16[256,1024]{1,0:T(8,128)(2,1)S(1)}, u32[]{:S(2)}, u32[]{:S(2)}) %collective-permute-start) | collective-permute-done | bytes 524320 | tf_op jit(solution)/shard_map/cond/branch_0_fun/ppermute | solution.py:680
  47.1 11.8 %collective-permute-done.1.before.refs_2_ = bf16[2752,128]{1,0:T(8,128)(2,1)S(1)} collective-permute-done((bf16[2752,128]{1,0:T(8,128)(2,1)}, bf16[2752,128]{1,0:T(8,128)(2,1)S(1)}, u32[]{:S(2)}, u32[]{:S(2)}) %collective-permute-start.1) | collective-permute-done | bytes 704544 | tf_op jit(solution)/shard_map/cond/branch_0_fun/ppermute | solution.py:611
  72.4 15.0 %collective-permute-done.2.b = bf16[256,1024]{1,0:T(8,128)(2,1)} collective-permute-done((bf16[256,1024]{1,0:T(8,128)(2,1)S(1)}, bf16[256,1024]{1,0:T(8,128)(2,1)}, u32[]{:S(2)}, u32[]{:S(2)}) %collective-permute-start.2) | collective-permute-done | bytes 524320 | tf_op jit(solution)/shard_map/cond/branch_0_fun/ppermute | solution.py:680
  93.8 14.3 %collective-permute-start.5 = (bf16[256,1024]{1,0:T(8,128)(2,1)}, bf16[256,1024]{1,0:T(8,128)(2,1)S(1)}, u32[]{:S(2)}, u32[]{:S(2)}) collective-permute-start(bf16[256,1024]{1,0:T(8,128)(2,1)} %either.16.after.a), channel_id=1, source_target_pairs={{0,8},{4,12},{16,24},{20,28},{1,9},{5,13},{17,25},{21,29},{2,10},{... | collective-permute-start | bytes 1572872 | tf_op jit(solution)/shard_map/cond/branch_0_fun/ppermute | solution.py:680
  121.6 10.9 %collective-permute-done.5.b = bf16[256,1024]{1,0:T(8,128)(2,1)S(1)} collective-permute-done((bf16[256,1024]{1,0:T(8,128)(2,1)}, bf16[256,1024]{1,0:T(8,128)(2,1)S(1)}, u32[]{:S(2)}, u32[]{:S(2)}) %collective-permute-start.5) | collective-permute-done | bytes 524320 | tf_op jit(solution)/shard_map/cond/branch_0_fun/ppermute | solution.py:680
  166.7 10.8 %collective-permute-done.9.refs_2_.low = bf16[128,2048]{1,0:T(8,128)(2,1)} collective-permute-done((bf16[128,2048]{1,0:T(8,128)(2,1)}, bf16[128,2048]{1,0:T(8,128)(2,1)}, u32[]{:S(2)}, u32[]{:S(2)}) %collective-permute-start.9) | collective-permute-done | bytes 524320 | tf_op jit(solution)/shard_map/cond/branch_0_fun/ppermute | solution.py:680
  177.5 17.6 %near_attend.3 = (f32[1024,1024]{1,0:T(8,128)}, f32[1024,128]{1,0:T(8,128)}) custom-call(s32[10,128]{1,0:T(8,128)S(1)} %get-tuple-element.56.lists.refs_0_, s32[2]{0:T(128)S(1)} %get-tuple-element.59.scal, bf16[256,1024]{1,0:T(8,128)(2,1)} %either.19.after.refs_5_.shared, bf16[1024,1024]{1,0:T(8,128)(2,1)} %get-tuple-element.125.q, ...), custom_call_target="tpu_custom_call" | custom-call | tf_op jit(solution)/shard_map/cond/branch_0_fun/near_attend/pallas_call | solution.py:482
  207.6 11.9 %collective-permute-done.13.refs_3_ = bf16[3392,128]{1,0:T(8,128)(2,1)S(1)} collective-permute-done((bf16[3392,128]{1,0:T(8,128)(2,1)}, bf16[3392,128]{1,0:T(8,128)(2,1)S(1)}, u32[]{:S(2)}, u32[]{:S(2)}) %collective-permute-start.13) | collective-permute-done | bytes 868384 | tf_op jit(solution)/shard_map/cond/branch_0_fun/ppermute | solution.py:611
  225.9 20.7 %collective-permute-done.15 = bf16[3776,128]{1,0:T(8,128)(2,1)} collective-permute-done((bf16[3776,128]{1,0:T(8,128)(2,1)}, bf16[3776,128]{1,0:T(8,128)(2,1)}, u32[]{:S(2)}, u32[]{:S(2)}) %collective-permute-start.15) | collective-permute-done | bytes 966688 | tf_op jit(solution)/shard_map/cond/branch_0_fun/ppermute | solution.py:611
  246.7 14.0 %far_scores.3 = (bf16[1024,3072]{1,0:T(8,128)(2,1)}, f32[1024,128]{1,0:T(8,128)}) custom-call(s32[10,128]{1,0:T(8,128)S(1)} %get-tuple-element.56.lists.refs_0_, s32[24,128]{1,0:T(8,128)S(1)} %get-tuple-element.58.table, bf16[3776,128]{1,0:T(8,128)(2,1)} %pack_tiles.47.after, bf16[1024,1024]{1,0:T(8,128)(2,1)} %get-tuple-element.125.q, ...), custom_call_target="tpu_custom_call" | custom-call | tf_op jit(solution)/shard_map/cond/branch_0_fun/far_scores/pallas_call | solution.py:540
  260.7 6.7 %collective-permute-done.16 = bf16[3776,128]{1,0:T(8,128)(2,1)} collective-permute-done((bf16[3776,128]{1,0:T(8,128)(2,1)}, bf16[3776,128]{1,0:T(8,128)(2,1)}, u32[]{:S(2)}, u32[]{:S(2)}) %collective-permute-start.16) | collective-permute-done | bytes 966688 | tf_op jit(solution)/shard_map/cond/branch_0_fun/ppermute | solution.py:611
  267.4 17.6 %collective-permute-done.17 = bf16[3776,128]{1,0:T(8,128)(2,1)S(1)} collective-permute-done((bf16[3776,128]{1,0:T(8,128)(2,1)}, bf16[3776,128]{1,0:T(8,128)(2,1)S(1)}, u32[]{:S(2)}, u32[]{:S(2)}) %collective-permute-start.17) | collective-permute-done | bytes 966688 | tf_op jit(solution)/shard_map/cond/branch_0_fun/ppermute | solution.py:611
  285.9 9.0 %far_values.9.refs_0_.refs_1_ = bf16[1024,512]{1,0:T(8,128)(2,1)} custom-call(s32[10,128]{1,0:T(8,128)S(1)} %get-tuple-element.56.lists.refs_0_, s32[24,128]{1,0:T(8,128)S(1)} %get-tuple-element.58.table, bf16[1024,3072]{1,0:T(8,128)(2,1)} %get-tuple-element.70.after.p, bf16[1024,3072]{1,0:T(8,128)(2,1)} %get-tuple-element.70.after.p, ...), custom_call_target="tpu_custom_call" | custom-call | tf_op jit(solution)/shard_map/cond/branch_0_fun/far_values/pallas_call | solution.py:597
  298.4 6.9 %far_values.10.refs_0_.refs_1_.refs_4_ = bf16[1024,256]{1,0:T(8,128)(2,1)} custom-call(s32[10,128]{1,0:T(8,128)S(1)} %get-tuple-element.56.lists.refs_0_, s32[24,128]{1,0:T(8,128)S(1)} %get-tuple-element.58.table, bf16[640,512]{1,0:T(8,128)(2,1)} %pack_blocks.27.after, bf16[1024,3072]{1,0:T(8,128)(2,1)} %get-tuple-element.70.after.p, ...), custom_call_target="tpu_custom_call" | custom-call | tf_op jit(solution)/shard_map/cond/branch_0_fun/far_values/pallas_call | solution.py:597
  307.2 6.9 %far_values.11.refs_0_.refs_1_.refs_8_ = bf16[1024,256]{1,0:T(8,128)(2,1)} custom-call(s32[10,128]{1,0:T(8,128)S(1)} %get-tuple-element.56.lists.refs_0_, s32[24,128]{1,0:T(8,128)S(1)} %get-tuple-element.58.table, bf16[640,256]{1,0:T(8,128)(2,1)} %pack_blocks.28.after, bf16[1024,3072]{1,0:T(8,128)(2,1)} %get-tuple-element.70.after.p, ...), custom_call_target="tpu_custom_call" | custom-call | tf_op jit(solution)/shard_map/cond/branch_0_fun/far_values/pallas_call | solution.py:597
  316.0 11.8 %collective-permute-done.18.refs_2_.refs_1_ = bf16[640,512]{1,0:T(8,128)(2,1)S(1)} collective-permute-done((bf16[640,512]{1,0:T(8,128)(2,1)}, bf16[640,512]{1,0:T(8,128)(2,1)S(1)}, u32[]{:S(2)}, u32[]{:S(2)}) %collective-permute-start.18) | collective-permute-done | bytes 655392 | tf_op jit(solution)/shard_map/cond/branch_0_fun/ppermute | solution.py:611
  333.6 10.9 %collective-permute-done.20.refs_2_.refs_5_ = bf16[640,256]{1,0:T(8,128)(2,1)S(1)} collective-permute-done((bf16[640,256]{1,0:T(8,128)(2,1)S(1)}, bf16[640,256]{1,0:T(8,128)(2,1)S(1)}, u32[]{:S(2)}, u32[]{:S(2)}) %collective-permute-start.20) | collective-permute-done | bytes 327712 | tf_op jit(solution)/shard_map/cond/branch_0_fun/ppermute | solution.py:611
  347.2 11.3 %collective-permute-done.19.refs_3_.refs_2_ = bf16[640,512]{1,0:T(8,128)(2,1)S(1)} collective-permute-done((bf16[640,512]{1,0:T(8,128)(2,1)}, bf16[640,512]{1,0:T(8,128)(2,1)S(1)}, u32[]{:S(2)}, u32[]{:S(2)}) %collective-permute-start.19) | collective-permute-done | bytes 655392 | tf_op jit(solution)/shard_map/cond/branch_0_fun/ppermute | solution.py:611
  367.6 5.8 %collective-permute-done.22.refs_3_.refs_6_ = bf16[640,256]{1,0:T(8,128)(2,1)S(1)} collective-permute-done((bf16[640,256]{1,0:T(8,128)(2,1)S(1)}, bf16[640,256]{1,0:T(8,128)(2,1)S(1)}, u32[]{:S(2)}, u32[]{:S(2)}) %collective-permute-start.22) | collective-permute-done | bytes 327712 | tf_op jit(solution)/shard_map/cond/branch_0_fun/ppermute | solution.py:611
  382.5 8.6 %collective-permute-done.24.refs_7_ = bf16[768,256]{1,0:T(8,128)(2,1)S(1)} collective-permute-done((bf16[768,256]{1,0:T(8,128)(2,1)}, bf16[768,256]{1,0:T(8,128)(2,1)S(1)}, u32[]{:S(2)}, u32[]{:S(2)}) %collective-permute-start.24) | collective-permute-done | bytes 393248 | tf_op jit(solution)/shard_map/cond/branch_0_fun/ppermute | solution.py:611
  391.1 6.6 %collective-permute-done.26.refs_11_ = bf16[768,256]{1,0:T(8,128)(2,1)S(1)} collective-permute-done((bf16[768,256]{1,0:T(8,128)(2,1)}, bf16[768,256]{1,0:T(8,128)(2,1)S(1)}, u32[]{:S(2)}, u32[]{:S(2)}) %collective-permute-start.26) | collective-permute-done | bytes 393248 | tf_op jit(solution)/shard_map/cond/branch_0_fun/ppermute | solution.py:611
  (141 shorter events, 150.7 us)
Async XLA Ops:
  24.9 34.0 %collective-permute-start.1 = (bf16[2752,128]{1,0:T(8,128)(2,1)}, bf16[2752,128]{1,0:T(8,128)(2,1)S(1)}, u32[]{:S(2)}, u32[]{:S(2)}) collective-permute-start(bf16[2752,128]{1,0:T(8,128)(2,1)} %pack_tiles.36.after), channel_id=1, source_target_pairs={{0,16},{4,20},{8,24},{12,28},{16,0},{20,4},{24,8},{28,12},{1,17},{... | collective-permute-start | bytes 2113544 | tf_op jit(solution)/shard_map/cond/branch_0_fun/ppermute | solution.py:611
  28.5 15.7 %collective-permute-start = (bf16[256,1024]{1,0:T(8,128)(2,1)}, bf16[256,1024]{1,0:T(8,128)(2,1)S(1)}, u32[]{:S(2)}, u32[]{:S(2)}) collective-permute-start(bf16[256,1024]{1,0:T(8,128)(2,1)} %get-tuple-element.65), channel_id=1, source_target_pairs={{0,4},{1,5},{2,6},{3,7}} | collective-permute-start | bytes 1572872 | tf_op jit(solution)/shard_map/cond/branch_0_fun/ppermute | solution.py:680
  59.7 31.2 %collective-permute-start.3 = (bf16[2752,128]{1,0:T(8,128)(2,1)}, bf16[2752,128]{1,0:T(8,128)(2,1)S(1)}, u32[]{:S(2)}, u32[]{:S(2)}) collective-permute-start(bf16[2752,128]{1,0:T(8,128)(2,1)} %hold.9.refs_0_), channel_id=1, source_target_pairs={{0,16},{4,20},{8,24},{12,28},{16,0},{20,4},{24,8},{28,12},{1,17},{... | collective-permute-start | bytes 2113544 | tf_op jit(solution)/shard_map/cond/branch_0_fun/ppermute | solution.py:611
  59.7 27.7 %collective-permute-start.2 = (bf16[256,1024]{1,0:T(8,128)(2,1)S(1)}, bf16[256,1024]{1,0:T(8,128)(2,1)}, u32[]{:S(2)}, u32[]{:S(2)}) collective-permute-start(bf16[256,1024]{1,0:T(8,128)(2,1)S(1)} %copy-done.25), channel_id=1, source_target_pairs={{0,16},{4,20},{1,17},{5,21},{2,18},{6,22},{3,19},{7,23}} | collective-permute-start | bytes 1572872 | tf_op jit(solution)/shard_map/cond/branch_0_fun/ppermute | solution.py:680
  69.4 47.4 %collective-permute-start.4 = (bf16[3392,128]{1,0:T(8,128)(2,1)}, bf16[3392,128]{1,0:T(8,128)(2,1)}, u32[]{:S(2)}, u32[]{:S(2)}) collective-permute-start(bf16[3392,128]{1,0:T(8,128)(2,1)} %pack_tiles.38.refs_0_), channel_id=1, source_target_pairs={{0,8},{4,12},{8,0},{12,4},{16,24},{20,28},{24,16},{28,20},{1,9},{5... | collective-permute-start | bytes 2605064 | tf_op jit(solution)/shard_map/cond/branch_0_fun/ppermute | solution.py:611
  91.8 43.5 %collective-permute-start.6 = (bf16[2752,128]{1,0:T(8,128)(2,1)}, bf16[2752,128]{1,0:T(8,128)(2,1)S(1)}, u32[]{:S(2)}, u32[]{:S(2)}) collective-permute-start(bf16[2752,128]{1,0:T(8,128)(2,1)} %hold.10.refs_0_), channel_id=1, source_target_pairs={{0,16},{4,20},{8,24},{12,28},{16,0},{20,4},{24,8},{28,12},{1,17},{... | collective-permute-start | bytes 2113544 | tf_op jit(solution)/shard_map/cond/branch_0_fun/ppermute | solution.py:611
  93.8 38.7 %collective-permute-start.5 = (bf16[256,1024]{1,0:T(8,128)(2,1)}, bf16[256,1024]{1,0:T(8,128)(2,1)S(1)}, u32[]{:S(2)}, u32[]{:S(2)}) collective-permute-start(bf16[256,1024]{1,0:T(8,128)(2,1)} %either.16.after.a), channel_id=1, source_target_pairs={{0,8},{4,12},{16,24},{20,28},{1,9},{5,13},{17,25},{21,29},{2,10},{... | collective-permute-start | bytes 1572872 | tf_op jit(solution)/shard_map/cond/branch_0_fun/ppermute | solution.py:680
  112.2 38.9 %collective-permute-start.7 = (bf16[3392,128]{1,0:T(8,128)(2,1)}, bf16[3392,128]{1,0:T(8,128)(2,1)}, u32[]{:S(2)}, u32[]{:S(2)}) collective-permute-start(bf16[3392,128]{1,0:T(8,128)(2,1)} %pack_tiles.40.refs_0_), channel_id=1, source_target_pairs={{0,8},{4,12},{8,0},{12,4},{16,24},{20,28},{24,16},{28,20},{1,9},{5... | collective-permute-start | bytes 2605064 | tf_op jit(solution)/shard_map/cond/branch_0_fun/ppermute | solution.py:611
  136.2 58.9 %collective-permute-start.11 = (bf16[2752,128]{1,0:T(8,128)(2,1)}, bf16[2752,128]{1,0:T(8,128)(2,1)S(1)}, u32[]{:S(2)}, u32[]{:S(2)}) collective-permute-start(bf16[2752,128]{1,0:T(8,128)(2,1)} %hold.11.refs_0_), channel_id=1, source_target_pairs={{0,16},{4,20},{8,24},{12,28},{16,0},{20,4},{24,8},{28,12},{1,17},{... | collective-permute-start | bytes 2113544 | tf_op jit(solution)/shard_map/cond/branch_0_fun/ppermute | solution.py:611
  136.2 26.3 %collective-permute-start.8 = (bf16[256,1024]{1,0:T(8,128)(2,1)}, bf16[256,1024]{1,0:T(8,128)(2,1)}, u32[]{:S(2)}, u32[]{:S(2)}) collective-permute-start(bf16[256,1024]{1,0:T(8,128)(2,1)} %either.17.after.a.b), channel_id=1, source_target_pairs={{0,4},{4,0},{8,12},{12,8},{16,20},{20,16},{24,28},{28,24},{1,5},{5... | collective-permute-start | bytes 1572872 | tf_op jit(solution)/shard_map/cond/branch_0_fun/ppermute | solution.py:611
  137.3 29.4 %collective-permute-start.10 = (bf16[128,2048]{1,0:T(8,128)(2,1)}, bf16[128,2048]{1,0:T(8,128)(2,1)S(1)}, u32[]{:S(2)}, u32[]{:S(2)}) collective-permute-start(bf16[128,2048]{1,0:T(8,128)(2,1)} %get-tuple-element.68), channel_id=1, source_target_pairs={{4,0},{8,4},{12,8},{16,12},{20,16},{24,20},{28,24},{5,1},{9,5},{13... | collective-permute-start | bytes 1572872 | tf_op jit(solution)/shard_map/cond/branch_0_fun/ppermute | solution.py:680
  140.2 37.3 %collective-permute-start.9 = (bf16[128,2048]{1,0:T(8,128)(2,1)}, bf16[128,2048]{1,0:T(8,128)(2,1)}, u32[]{:S(2)}, u32[]{:S(2)}) collective-permute-start(bf16[128,2048]{1,0:T(8,128)(2,1)} %get-tuple-element.62.refs_0_), channel_id=1, source_target_pairs={{0,4},{4,8},{8,12},{12,16},{16,20},{20,24},{24,28},{1,5},{5,9},{9,... | collective-permute-start | bytes 1572872 | tf_op jit(solution)/shard_map/cond/branch_0_fun/ppermute | solution.py:680
  151.1 52.3 %collective-permute-start.12 = (bf16[3392,128]{1,0:T(8,128)(2,1)}, bf16[3392,128]{1,0:T(8,128)(2,1)}, u32[]{:S(2)}, u32[]{:S(2)}) collective-permute-start(bf16[3392,128]{1,0:T(8,128)(2,1)} %pack_tiles.43.refs_0_), channel_id=1, source_target_pairs={{0,8},{4,12},{8,0},{12,4},{16,24},{20,28},{24,16},{28,20},{1,9},{5... | collective-permute-start | bytes 2605064 | tf_op jit(solution)/shard_map/cond/branch_0_fun/ppermute | solution.py:611
  199.4 20.1 %collective-permute-start.13 = (bf16[3392,128]{1,0:T(8,128)(2,1)}, bf16[3392,128]{1,0:T(8,128)(2,1)S(1)}, u32[]{:S(2)}, u32[]{:S(2)}) collective-permute-start(bf16[3392,128]{1,0:T(8,128)(2,1)} %pack_tiles.45.refs_0_), channel_id=1, source_target_pairs={{0,8},{4,12},{8,0},{12,4},{16,24},{20,28},{24,16},{28,20},{1,9},{5... | collective-permute-start | bytes 2605064 | tf_op jit(solution)/shard_map/cond/branch_0_fun/ppermute | solution.py:611
  201.4 24.6 %collective-permute-start.14 = (bf16[3776,128]{1,0:T(8,128)(2,1)}, bf16[3776,128]{1,0:T(8,128)(2,1)}, u32[]{:S(2)}, u32[]{:S(2)}) collective-permute-start(bf16[3776,128]{1,0:T(8,128)(2,1)} %pack_tiles.42.after), channel_id=1, source_target_pairs={{0,4},{4,0},{8,12},{12,8},{16,20},{20,16},{24,28},{28,24},{1,5},{5... | collective-permute-start | bytes 2899976 | tf_op jit(solution)/shard_map/cond/branch_0_fun/ppermute | solution.py:611
  201.4 45.3 %collective-permute-start.15 = (bf16[3776,128]{1,0:T(8,128)(2,1)}, bf16[3776,128]{1,0:T(8,128)(2,1)}, u32[]{:S(2)}, u32[]{:S(2)}) collective-permute-start(bf16[3776,128]{1,0:T(8,128)(2,1)} %pack_tiles.44.after), channel_id=1, source_target_pairs={{0,4},{4,0},{8,12},{12,8},{16,20},{20,16},{24,28},{28,24},{1,5},{5... | collective-permute-start | bytes 2899976 | tf_op jit(solution)/shard_map/cond/branch_0_fun/ppermute | solution.py:611
  207.5 59.9 %collective-permute-start.16 = (bf16[3776,128]{1,0:T(8,128)(2,1)}, bf16[3776,128]{1,0:T(8,128)(2,1)}, u32[]{:S(2)}, u32[]{:S(2)}) collective-permute-start(bf16[3776,128]{1,0:T(8,128)(2,1)} %pack_tiles.46.refs_0_), channel_id=1, source_target_pairs={{0,4},{4,0},{8,12},{12,8},{16,20},{20,16},{24,28},{28,24},{1,5},{5... | collective-permute-start | bytes 2899976 | tf_op jit(solution)/shard_map/cond/branch_0_fun/ppermute | solution.py:611
  224.6 60.4 %collective-permute-start.17 = (bf16[3776,128]{1,0:T(8,128)(2,1)}, bf16[3776,128]{1,0:T(8,128)(2,1)S(1)}, u32[]{:S(2)}, u32[]{:S(2)}) collective-permute-start(bf16[3776,128]{1,0:T(8,128)(2,1)} %pack_tiles.47.after), channel_id=1, source_target_pairs={{0,4},{4,0},{8,12},{12,8},{16,20},{20,16},{24,28},{28,24},{1,5},{5... | collective-permute-start | bytes 2899976 | tf_op jit(solution)/shard_map/cond/branch_0_fun/ppermute | solution.py:611
  297.1 30.7 %collective-permute-start.18 = (bf16[640,512]{1,0:T(8,128)(2,1)}, bf16[640,512]{1,0:T(8,128)(2,1)S(1)}, u32[]{:S(2)}, u32[]{:S(2)}) collective-permute-start(bf16[640,512]{1,0:T(8,128)(2,1)} %pack_blocks.27.after), channel_id=1, source_target_pairs={{16,0},{20,4},{24,8},{28,12},{17,1},{21,5},{25,9},{29,13},{18,2},{... | collective-permute-start | bytes 1966088 | tf_op jit(solution)/shard_map/cond/branch_0_fun/ppermute | solution.py:611
  331.0 27.5 %collective-permute-start.19 = (bf16[640,512]{1,0:T(8,128)(2,1)}, bf16[640,512]{1,0:T(8,128)(2,1)S(1)}, u32[]{:S(2)}, u32[]{:S(2)}) collective-permute-start(bf16[640,512]{1,0:T(8,128)(2,1)} %pack_blocks.30.refs_0_), channel_id=1, source_target_pairs={{0,8},{4,12},{8,0},{12,4},{16,24},{20,28},{24,16},{28,20},{1,9},{5... | collective-permute-start | bytes 1966088 | tf_op jit(solution)/shard_map/cond/branch_0_fun/ppermute | solution.py:611
  332.3 32.2 %collective-permute-start.23 = (bf16[640,256]{1,0:T(8,128)(2,1)S(1)}, bf16[640,256]{1,0:T(8,128)(2,1)S(1)}, u32[]{:S(2)}, u32[]{:S(2)}) collective-permute-start(bf16[640,256]{1,0:T(8,128)(2,1)S(1)} %copy-done.48), channel_id=1, source_target_pairs={{16,0},{20,4},{24,8},{28,12},{17,1},{21,5},{25,9},{29,13},{18,2},{... | collective-permute-start | bytes 983048 | tf_op jit(solution)/shard_map/cond/branch_0_fun/ppermute | solution.py:611
  362.1 35.7 %collective-permute-start.21 = (bf16[768,512]{1,0:T(8,128)(2,1)}, bf16[768,512]{1,0:T(8,128)(2,1)S(1)}, u32[]{:S(2)}, u32[]{:S(2)}) collective-permute-start(bf16[768,512]{1,0:T(8,128)(2,1)} %pack_blocks.32.refs_0_), channel_id=1, source_target_pairs={{0,4},{4,0},{8,12},{12,8},{16,20},{20,16},{24,28},{28,24},{1,5},{5... | collective-permute-start | bytes 2359304 | tf_op jit(solution)/shard_map/cond/branch_0_fun/ppermute | solution.py:611
  376.4 14.8 %collective-permute-start.24 = (bf16[768,256]{1,0:T(8,128)(2,1)}, bf16[768,256]{1,0:T(8,128)(2,1)S(1)}, u32[]{:S(2)}, u32[]{:S(2)}) collective-permute-start(bf16[768,256]{1,0:T(8,128)(2,1)} %pack_blocks.34.refs_0_), channel_id=1, source_target_pairs={{0,4},{4,0},{8,12},{12,8},{16,20},{20,16},{24,28},{28,24},{1,5},{5... | collective-permute-start | bytes 1179656 | tf_op jit(solution)/shard_map/cond/branch_0_fun/ppermute | solution.py:611
  381.5 16.2 %collective-permute-start.26 = (bf16[768,256]{1,0:T(8,128)(2,1)}, bf16[768,256]{1,0:T(8,128)(2,1)S(1)}, u32[]{:S(2)}, u32[]{:S(2)}) collective-permute-start(bf16[768,256]{1,0:T(8,128)(2,1)} %pack_blocks.35), channel_id=1, source_target_pairs={{0,4},{4,0},{8,12},{12,8},{16,20},{20,16},{24,28},{28,24},{1,5},{5... | collective-permute-start | bytes 1179656 | tf_op jit(solution)/shard_map/cond/branch_0_fun/ppermute | solution.py:611
  (29 other events, 158.3 us)
where the time goes:
time: 410 us; the launch traced here: 404 us
  waiting for transfers between devices  192 us (47%)
  Pallas kernels  138 us (34%)
  starting transfers between devices  52.5 us (13%)
  local copies, waits for them, and re-layouts  18.1 us (4%)
    ppermute x22, waiting for transfers between devices, swap(): return lax.ppermute(x, 'seq', pairs)  138 us
    pallas_call x21, Pallas kernels, pack(): pl.pallas_call(functools.partial(pack_body, row, size, bases, own_part, r...  63.9 us
    ppermute x5, waiting for transfers between devices, hop(): return lax.ppermute(x, 'seq', pairs)  47.8 us
    ppermute x5, starting transfers between devices, hop(): return lax.ppermute(x, 'seq', pairs)  29 us
    pallas_call x3, Pallas kernels, far_values(): pl.pallas_call(functools.partial(far_values_body, plan, sizes, heads), ou...  22.8 us
    pallas_call x1, Pallas kernels, near_attend(): pl.pallas_call(functools.partial(near_body, plan), out_shape=(jax.ShapeDt...  17.6 us
    ppermute x22, starting transfers between devices, swap(): return lax.ppermute(x, 'seq', pairs)  17.4 us
    pallas_call x1, Pallas kernels, far_scores(): pl.pallas_call(functools.partial(far_scores_body, plan, sizes), out_shape...  14 us
  transfers between devices with their start and end apart: 28, of which 23 were waited for; matrix products, arithmetic and copies ran while one was open for 0% of the time, Pallas kernels for 28%

commit v1 on v0

--- a/solution.py
+++ b/solution.py
@@ -8,6 +8,7 @@
 from jax.experimental.pallas import tpu as pltpu
 from jax.sharding import PartitionSpec as P
 
+
 DH = 128
 B = 128
 G = 2
@@ -19,7 +20,8 @@
 ROUTE_SHARES = ((0.66, 0.545, 0.61), (0.73, 0.6, 0.7), (1.0, 1.0, 1.0))
 PACK_SHARES = ((0.7, 0.35, 0.75), (0.8, 0.45, 0.85), (1.0, 1.0, 1.0))
 PARTS = 2
-SPLIT = (4, 6)
+UNROLL = 4
+SPLIT = (2, 4, 6)
 
 
 def log2(size):
@@ -41,7 +43,6 @@
         bound = (count // 2) * most * head_dev
         self.full = [min(self.own << s, bound) for s in range(self.bits)]
         self.base = [sum(self.full[:s]) for s in range(self.bits)]
-        self.pool = head_dev * self.per_head + sum(self.full)
         self.cfull = [
             min((blk_dev - 1) << s, blk_dev << (self.bits - 1 - s)) for s in range(self.bits)
         ]
@@ -248,13 +249,12 @@
     lax.fori_loop(0, size, step, 0)
 
 
-def pack(row, size, bases, own_part, rows, lists, after, sources, width, name):
+def pack(row, size, bases, own_part, rows, lists, after, sources, width):
     return pl.pallas_call(
         functools.partial(pack_body, row, size, bases, own_part, rows),
         out_shape=jax.ShapeDtypeStruct((size * rows, width), jnp.bfloat16),
         in_specs=[SMEM, ANY] + [VMEM] * len(sources),
         out_specs=VMEM,
-        name=name,
     )(lists, after, *sources)
 
 
@@ -440,12 +440,12 @@
     stat[rows, :] = jnp.where(lane == h, top, jnp.where(lane == hd + h, total, old))
 
 
-def near_body(plan, lists, scal, after, q, *refs):
+def near_body(plan, heads, lists, scal, after, q, *refs):
     k, v, low, high, shared_k, shared_v, acc_out, stat_out, kp, vp, sem = refs
     blk, hd, per = plan.blk, plan.heads, plan.per_head
     copies = []
-    start_near(plan, range(hd), k, low, high, shared_k, 0, kp, sem, copies)
-    start_near(plan, range(hd), v, low, high, shared_v, 1, vp, sem, copies)
+    start_near(plan, heads, k, low, high, shared_k, 0, kp, sem, copies)
+    start_near(plan, heads, v, low, high, shared_v, 1, vp, sem, copies)
     for copy in copies:
         copy.wait()
     me = scal[0]
@@ -459,7 +459,7 @@
         col = lax.broadcasted_iota(jnp.int32, (B, win), 1)
         dead = (first & (col < B)) | (last & (col >= 2 * B))
         rows = pl.ds(pl.multiple_of(i * B, B), B)
-        for h in range(hd):
+        for number, h in enumerate(heads):
             qt = q[rows, h * DH : (h + 1) * DH]
             spans = (
                 pl.ds(pl.multiple_of((h * per + i) * B, B), win),
@@ -469,7 +469,7 @@
             scores[0] = jnp.where(dead, neg_big, scores[0])
             top = peak(scores)
             total, acc = gather_parts(scores, [vp[span, :] for span in spans], top)
-            acc_out[rows, h * DH : (h + 1) * DH] = acc
+            acc_out[rows, number * DH : (number + 1) * DH] = acc
             stat_out[rows, h : h + 1] = top
             stat_out[rows, hd + h : hd + h + 1] = total
         return carry
@@ -477,12 +477,12 @@
     lax.fori_loop(0, lists[row + 3, 0], step, 0)
 
 
-def near_attend(plan, lists, scal, after, q, ins):
+def near_attend(plan, heads, lists, scal, after, q, ins):
     pool = plan.heads * plan.per_head * B
     return pl.pallas_call(
-        functools.partial(near_body, plan),
+        functools.partial(near_body, plan, heads),
         out_shape=(
-            jax.ShapeDtypeStruct(q.shape, jnp.float32),
+            jax.ShapeDtypeStruct((q.shape[0], len(heads) * DH), jnp.float32),
             jax.ShapeDtypeStruct((q.shape[0], LANES), jnp.float32),
         ),
         in_specs=[SMEM, SMEM, ANY, VMEM] + [HBM] * len(ins),
@@ -510,20 +510,26 @@
     def step(kk, carry):
         i = lists[row + 2, kk]
         rows = pl.ds(pl.multiple_of(i * B, B), B)
-        for h in range(hd):
-            qt = q[rows, h * DH : (h + 1) * DH]
-            scores = [
-                scores_of(qt, tile_reader(plan, near, far, table[i * R + r, h])) for r in range(R)
-            ]
-            top = peak(scores)
-            total = 0.0
-            for r, s in enumerate(scores):
-                p = jnp.exp2((s - top) * FACTOR)
-                total = total + jnp.sum(p, axis=1, keepdims=True)
-                p_out[rows, (h * R + r) * B : (h * R + r + 1) * B] = p.astype(jnp.bfloat16)
-            stat_out[rows, h : h + 1] = top
-            stat_out[rows, hd + h : hd + h + 1] = total
-        return carry
+
+        def some_heads(g, carry):
+            for n in range(UNROLL):
+                h = g * UNROLL + n
+                qt = q[rows, pl.ds(pl.multiple_of(h * DH, DH), DH)]
+                scores = [
+                    scores_of(qt, tile_reader(plan, near, far, table[i * R + r, h]))
+                    for r in range(R)
+                ]
+                top = peak(scores)
+                total = 0.0
+                for r, s in enumerate(scores):
+                    p = jnp.exp2((s - top) * FACTOR)
+                    total = total + jnp.sum(p, axis=1, keepdims=True)
+                    at = pl.multiple_of((h * R + r) * B, B)
+                    p_out[rows, pl.ds(at, B)] = p.astype(jnp.bfloat16)
+                put_stats(stat_out, rows, hd, h, top, total)
+            return carry
+
+        return lax.fori_loop(0, hd // UNROLL, some_heads, carry)
 
     lax.fori_loop(0, lists[row + 3, 0], step, 0)
 
@@ -589,26 +595,23 @@
 def far_values(plan, sizes, heads, lists, table, after, p, pstat, acc, stat, v, low, high, shared,
                chunks):
     size = len(heads)
-    assert heads[0] % size == 0
-
-    def of_team(x, width):
-        return pl.BlockSpec((x.shape[0], size * width), lambda _: (0, heads[0] // size))
+    half = acc.shape[1] // DH
+    assert heads[0] % size == 0 and half % size == 0
+
+    def of_team(x, width, first):
+        return pl.BlockSpec((x.shape[0], size * width), lambda _: (0, first // size))
 
     return pl.pallas_call(
         functools.partial(far_values_body, plan, sizes, heads),
         out_shape=jax.ShapeDtypeStruct((p.shape[0], len(heads) * DH), jnp.bfloat16),
         grid=(1,),
-        in_specs=[SMEM, SMEM, ANY, of_team(p, R * B), VMEM, of_team(acc, DH), VMEM]
+        in_specs=[SMEM, SMEM, ANY, of_team(p, R * B, heads[0]), VMEM,
+                  of_team(acc, DH, heads[0] % half), VMEM]
         + [HBM] * (4 + len(chunks)),
         out_specs=VMEM,
         scratch_shapes=pools_of(plan),
         name="far_values",
     )(lists, table, after, p, pstat, acc, stat, v, low, high, shared, *chunks)
-
-
-def swap(x, bit, count, down_only=False):
-    pairs = [(i, i ^ bit) for i in range(count) if not down_only or i & bit]
-    return lax.ppermute(x, "seq", pairs)
 
 
 def body(queries, keys, values, random_holder, random_offset, keep):
@@ -636,14 +639,12 @@
     rows = B // PARTS
     row = 2 * bits
     cuts = [0] + [cut for cut in SPLIT if cut < head_dev] + [head_dev]
-    if len(cuts) == 2:
-        cuts = [0, head_dev // 2, head_dev]
     teams = [range(low, high) for low, high in zip(cuts, cuts[1:])]
     flags = lambda cond: jnp.concatenate((scal, cond.astype(jnp.int32)[None]))
     odd = flags((me & 1) == 1)
 
     def branch(sizes, csizes):
-        def run(queries, keys, values, lists, table, scal, odd):
+        def steps(queries, keys, values, lists, table, scal, odd):
             got = [[] for _ in range(2 * PARTS)]
             last = [lists]
 
@@ -651,6 +652,12 @@
                 out = fn(last[0], *args)
                 last[0] = out[0] if isinstance(out, (tuple, list)) else out
                 return out
+
+            def hop(x, pairs):
+                return lax.ppermute(x, "seq", pairs)
+
+            def swap(x, bit, count, down_only=False):
+                return hop(x, [(i, i ^ bit) for i in range(count) if not down_only or i & bit])
 
             def packed_tiles(s, chunk):
                 which, part = chunk // PARTS, chunk % PARTS
@@ -658,7 +665,7 @@
                 return run_after(
                     lambda after: pack(
                         s, sizes[s], bases, tile_part(blk_bits, part, rows), rows, lists, after,
-                        [(keys, values)[which]] + got[chunk], DH, "pack_tiles",
+                        [(keys, values)[which]] + got[chunk], DH,
                     )
                 )
 
@@ -675,9 +682,6 @@
             def begin(chunk, packed):
                 packed = run_after(lambda after: hold(after, got[chunk - 1][0], packed))
                 got[chunk].append(swap(packed, count >> 1, count))
-
-            def hop(x, pairs):
-                return lax.ppermute(x, "seq", pairs)
 
             stage(0, 0)
             low, high, first_keys, first_values = run_after(edges, keys, values)
@@ -693,6 +697,18 @@
                     (bit, [(i + j, i + j + bit) for i in range(0, count, 2 * bit) for j in (0, 1)])
                 )
             chunks = 2 * PARTS
+            last_spread = max(len(spreads), chunks - 2)
+            nears = []
+
+            def near_half(number):
+                half = head_dev // 2
+                return run_after(
+                    lambda after: near_attend(
+                        plan, range(number * half, (number + 1) * half), lists, scal, after,
+                        queries, [keys, values, low, high, shared_keys, shared_values],
+                    )
+                )
+
             for step in range(chunks + bits - 1):
                 there = None
                 if step < len(spreads):
@@ -703,6 +719,8 @@
                 if step + 1 < chunks:
                     begin(step + 1, coming)
                 for s in range(1, bits):
+                    if s == 2 and step == max(chunks - 1, len(spreads) + 1):
+                        nears.append(near_half(1))
                     if 0 <= step + 1 - s < chunks:
                         stage(s, step + 1 - s)
                     if s == 1 and step + 2 < chunks:
@@ -712,20 +730,19 @@
                 elif step == len(spreads):
                     shared_keys = run_after(either, odd, held, there)
                     shared_values = run_after(either, odd, there, held)
-                if step == max(len(spreads), chunks - 2):
-                    acc, stat = run_after(
-                        lambda after: near_attend(
-                            plan, lists, scal, after, queries,
-                            [keys, values, low, high, shared_keys, shared_values],
-                        )
-                    )
-                if step == chunks + bits - 3:
+                if step == 1:
+                    low = run_after(hold, high, low)
+                if step == last_spread:
+                    nears.append(near_half(0))
+                if step == max(chunks, last_spread):
                     p, pstat = run_after(
                         lambda after: far_scores(
                             plan, sizes, lists, table, after, queries, keys, low, high,
                             shared_keys, tiles(0),
                         )
                     )
+            if len(nears) == 1:
+                nears.append(near_half(1))
 
             sources = []
 
@@ -734,12 +751,13 @@
                 packed = run_after(
                     lambda after: pack(
                         bits + s, csizes[s], bases, block_part, B, lists, after, held,
-                        held[0].shape[1], "pack_blocks",
+                        held[0].shape[1],
                     )
                 )
                 held.append(swap(packed, count >> (s + 1), count, s == 0))
 
             for half, heads in enumerate(teams):
+                acc, stat = nears[heads[0] // (head_dev // 2)]
                 attended = run_after(
                     lambda after: far_values(
                         plan, sizes, heads, lists, table, after, p, pstat, acc, stat, values,
@@ -756,7 +774,7 @@
             widths = [len(heads) * DH for heads in teams]
             return final(row, blk_dev, bases, lists, sum(sources, []), widths)
 
-        return run
+        return steps
 
     return lax.switch(
         lists[row + 1, 0],

time: 410 us -> 449 us (1.095)
  starting transfers between devices: 52.5 us -> 73.3 us
  waiting for transfers between devices: 192 us -> 203 us
  Pallas kernels: 138 us -> 146 us
    ppermute x5 -> x30, waiting for transfers between devices: 47.8 us -> 197 us  [hop(): return lax.ppermute(x, 'seq', pairs)]
    ppermute x22 -> x0, waiting for transfers between devices: 138 us -> none  [swap(): return lax.ppermute(x, 'seq', pairs)]
    ppermute x5 -> x30, starting transfers between devices: 29 us -> 67.1 us  [hop(): return lax.ppermute(x, 'seq', pairs)]
    ppermute x22 -> x0, starting transfers between devices: 17.4 us -> none  [swap(): return lax.ppermute(x, 'seq', pairs)]
    pallas_call x21 -> x24, Pallas kernels: 63.9 us -> 72.6 us  [pack(): pl.pallas_call(functools.partial(pack_body, row, size, bases, own_part, r...]
    pallas_call x3 -> x4, Pallas kernels: 22.8 us -> 25.9 us  [far_values(): pl.pallas_call(functools.partial(far_values_body, plan, sizes, heads), ou...]
    pallas_call x1 -> x2, Pallas kernels: 17.6 us -> 16.4 us  [near_attend(): pl.pallas_call(functools.partial(near_body, plan, heads), out_shape=(jax....]
    cond x46 -> x54, local copies, waits for them, and re-layouts: 13.1 us -> 14.2 us
  transfers between devices with their start and end apart: 28 -> 31, of which waited for: 23 -> 21; matrix products, arithmetic and copies ran while one was open for 0% -> 0% of each run, Pallas kernels for 28% -> 29%
where the time goes in v1:
time: 449 us; the launch traced here: 445 us
  waiting for transfers between devices  203 us (45%)
  Pallas kernels  146 us (33%)
  starting transfers between devices  73.3 us (16%)
  local copies, waits for them, and re-layouts  19.1 us (4%)
    ppermute x30, waiting for transfers between devices, hop(): return lax.ppermute(x, 'seq', pairs)  197 us
    pallas_call x24, Pallas kernels, pack(): pl.pallas_call(functools.partial(pack_body, row, size, bases, own_part, r...  72.6 us
    ppermute x30, starting transfers between devices, hop(): return lax.ppermute(x, 'seq', pairs)  67.1 us
    pallas_call x4, Pallas kernels, far_values(): pl.pallas_call(functools.partial(far_values_body, plan, sizes, heads), ou...  25.9 us
    pallas_call x2, Pallas kernels, near_attend(): pl.pallas_call(functools.partial(near_body, plan, heads), out_shape=(jax....  16.4 us
    cond x54, local copies, waits for them, and re-layouts  14.2 us
    pallas_call x1, Pallas kernels, far_scores(): pl.pallas_call(functools.partial(far_scores_body, plan, sizes), out_shape...  11.4 us
    pallas_call x5, Pallas kernels, either(): pl.pallas_call(either_body, out_shape=jax.ShapeDtypeStruct(a.shape, a.dty...  10.3 us
  transfers between devices with their start and end apart: 31, of which 21 were waited for; matrix products, arithmetic and copies ran while one was open for 0% of the time, Pallas kernels for 29%

profile of v1, /device:TPU:2, one launch (start us, length us, event | category | flops | bytes accessed | tf_op | source)
XLA Modules:
  0.0 445.2 jit_solution(1261263309965011002)
XLA Ops:
  21.4 422.5 %conditional.1 = (bf16[1024,1024]{1,0:T(8,128)(2,1)S(1)}) conditional(s32[]{:T(128)} %bitcast.47, (s32[10,128]{1,0:T(8,128)S(1)}, bf16[1024,1024]{1,0:T(8,128)(2,1)}, bf16[1024,1024]{1,0:T(8,128)(2,1)}, s32[3]{0:T(128)S(1)}, s32[]{:T(128)}, /*index=5*/s32[2]{0:T(128)S(1)}, bf16[1024,1024]{1,0:T(8,128)(2,1)}, ...), branch_computations={%region_0.1_spmd, %region_1.2_spmd, %region_2.3_spmd} | conditional | flops 12 | bytes 169608960 | solution.py:779
  33.5 11.0 %collective-permute-done.30.b = bf16[256,1024]{1,0:T(8,128)(2,1)S(1)} collective-permute-done((bf16[256,1024]{1,0:T(8,128)(2,1)}, bf16[256,1024]{1,0:T(8,128)(2,1)S(1)}, u32[]{:S(2)}, u32[]{:S(2)}) %collective-permute-start.30) | collective-permute-done | bytes 524320 | tf_op jit(solution)/shard_map/cond/branch_1_fun/ppermute | solution.py:657
  47.4 14.6 %collective-permute-done.31.before.refs_2_ = bf16[3008,128]{1,0:T(8,128)(2,1)S(1)} collective-permute-done((bf16[3008,128]{1,0:T(8,128)(2,1)}, bf16[3008,128]{1,0:T(8,128)(2,1)S(1)}, u32[]{:S(2)}, u32[]{:S(2)}) %collective-permute-start.31) | collective-permute-done | bytes 770080 | tf_op jit(solution)/shard_map/cond/branch_1_fun/ppermute | solution.py:657
  75.8 16.1 %collective-permute-done.32.b = bf16[256,1024]{1,0:T(8,128)(2,1)} collective-permute-done((bf16[256,1024]{1,0:T(8,128)(2,1)S(1)}, bf16[256,1024]{1,0:T(8,128)(2,1)}, u32[]{:S(2)}, u32[]{:S(2)}) %collective-permute-start.32) | collective-permute-done | bytes 524320 | tf_op jit(solution)/shard_map/cond/branch_1_fun/ppermute | solution.py:657
  98.4 16.5 %collective-permute-start.35 = (bf16[256,1024]{1,0:T(8,128)(2,1)}, bf16[256,1024]{1,0:T(8,128)(2,1)}, u32[]{:S(2)}, u32[]{:S(2)}) collective-permute-start(bf16[256,1024]{1,0:T(8,128)(2,1)} %either.21.after.a), channel_id=1, source_target_pairs={{0,8},{4,12},{16,24},{20,28},{1,9},{5,13},{17,25},{21,29},{2,10},{... | collective-permute-start | bytes 1572872 | tf_op jit(solution)/shard_map/cond/branch_1_fun/ppermute | solution.py:657
  133.5 6.7 %collective-permute-done.35.b = bf16[256,1024]{1,0:T(8,128)(2,1)} collective-permute-done((bf16[256,1024]{1,0:T(8,128)(2,1)}, bf16[256,1024]{1,0:T(8,128)(2,1)}, u32[]{:S(2)}, u32[]{:S(2)}) %collective-permute-start.35) | collective-permute-done | bytes 524320 | tf_op jit(solution)/shard_map/cond/branch_1_fun/ppermute | solution.py:657
  142.2 9.2 %collective-permute-done.37.x = bf16[128,2048]{1,0:T(8,128)(2,1)S(1)} collective-permute-done((bf16[128,2048]{1,0:T(8,128)(2,1)}, bf16[128,2048]{1,0:T(8,128)(2,1)S(1)}, u32[]{:S(2)}, u32[]{:S(2)}) %collective-permute-start.37) | collective-permute-done | bytes 524320 | tf_op jit(solution)/shard_map/cond/branch_1_fun/ppermute | solution.py:657
  164.1 7.7 %collective-permute-done.39.refs_3_ = bf16[3712,128]{1,0:T(8,128)(2,1)} collective-permute-done((bf16[3712,128]{1,0:T(8,128)(2,1)}, bf16[3712,128]{1,0:T(8,128)(2,1)}, u32[]{:S(2)}, u32[]{:S(2)}) %collective-permute-start.39) | collective-permute-done | bytes 950304 | tf_op jit(solution)/shard_map/cond/branch_1_fun/ppermute | solution.py:657
  181.1 8.2 %near_attend.8 = (f32[1024,512]{1,0:T(8,128)}, f32[1024,128]{1,0:T(8,128)}) custom-call(s32[10,128]{1,0:T(8,128)S(1)} %get-tuple-element.75.lists.refs_0_, s32[2]{0:T(128)S(1)} %get-tuple-element.77.scal, bf16[256,1024]{1,0:T(8,128)(2,1)} %either.24.after.refs_5_.shared, bf16[1024,1024]{1,0:T(8,128)(2,1)} %get-tuple-element.132.q, ...), custom_call_target="tpu_custom_call" | custom-call | tf_op jit(solution)/shard_map/cond/branch_1_fun/near_attend/pallas_call | solution.py:482
  201.2 8.2 %near_attend.9 = (f32[1024,512]{1,0:T(8,128)}, f32[1024,128]{1,0:T(8,128)}) custom-call(s32[10,128]{1,0:T(8,128)S(1)} %get-tuple-element.75.lists.refs_0_, s32[2]{0:T(128)S(1)} %get-tuple-element.77.scal, bf16[3712,128]{1,0:T(8,128)(2,1)} %branch_1_fun.33.after, bf16[1024,1024]{1,0:T(8,128)(2,1)} %get-tuple-element.132.q, ...), custom_call_target="tpu_custom_call" | custom-call | tf_op jit(solution)/shard_map/cond/branch_1_fun/near_attend/pallas_call | solution.py:482
  217.0 11.3 %collective-permute-done.43.refs_3_ = bf16[3712,128]{1,0:T(8,128)(2,1)S(1)} collective-permute-done((bf16[3712,128]{1,0:T(8,128)(2,1)}, bf16[3712,128]{1,0:T(8,128)(2,1)S(1)}, u32[]{:S(2)}, u32[]{:S(2)}) %collective-permute-start.43) | collective-permute-done | bytes 950304 | tf_op jit(solution)/shard_map/cond/branch_1_fun/ppermute | solution.py:657
  233.9 16.9 %collective-permute-done.45 = bf16[4352,128]{1,0:T(8,128)(2,1)} collective-permute-done((bf16[4352,128]{1,0:T(8,128)(2,1)}, bf16[4352,128]{1,0:T(8,128)(2,1)}, u32[]{:S(2)}, u32[]{:S(2)}) %collective-permute-start.45) | collective-permute-done | bytes 1114144 | tf_op jit(solution)/shard_map/cond/branch_1_fun/ppermute | solution.py:657
  250.8 11.4 %far_scores.4 = (bf16[1024,3072]{1,0:T(8,128)(2,1)}, f32[1024,128]{1,0:T(8,128)}) custom-call(s32[10,128]{1,0:T(8,128)S(1)} %get-tuple-element.75.lists.refs_0_, s32[24,128]{1,0:T(8,128)S(1)} %get-tuple-element.76.table, bf16[4352,128]{1,0:T(8,128)(2,1)} %branch_1_fun.35.after, bf16[1024,1024]{1,0:T(8,128)(2,1)} %get-tuple-element.132.q, ...), custom_call_target="tpu_custom_call" | custom-call | tf_op jit(solution)/shard_map/cond/branch_1_fun/far_scores/pallas_call | solution.py:546
  262.2 12.5 %collective-permute-done.46 = bf16[4352,128]{1,0:T(8,128)(2,1)} collective-permute-done((bf16[4352,128]{1,0:T(8,128)(2,1)}, bf16[4352,128]{1,0:T(8,128)(2,1)}, u32[]{:S(2)}, u32[]{:S(2)}) %collective-permute-start.46) | collective-permute-done | bytes 1114144 | tf_op jit(solution)/shard_map/cond/branch_1_fun/ppermute | solution.py:657
  274.7 21.2 %collective-permute-done.47 = bf16[4352,128]{1,0:T(8,128)(2,1)S(1)} collective-permute-done((bf16[4352,128]{1,0:T(8,128)(2,1)}, bf16[4352,128]{1,0:T(8,128)(2,1)S(1)}, u32[]{:S(2)}, u32[]{:S(2)}) %collective-permute-start.47) | collective-permute-done | bytes 1114144 | tf_op jit(solution)/shard_map/cond/branch_1_fun/ppermute | solution.py:657
  296.9 6.4 %far_values.16.refs_0_.refs_1_ = bf16[1024,256]{1,0:T(8,128)(2,1)} custom-call(s32[10,128]{1,0:T(8,128)S(1)} %get-tuple-element.75.lists.refs_0_, s32[24,128]{1,0:T(8,128)S(1)} %get-tuple-element.76.table, bf16[1024,3072]{1,0:T(8,128)(2,1)} %get-tuple-element.89.after.p, bf16[1024,3072]{1,0:T(8,128)(2,1)} %get-tuple-element.89.after.p, ...), custom_call_target="tpu_custom_call" | custom-call | tf_op jit(solution)/shard_map/cond/branch_1_fun/far_values/pallas_call | solution.py:604
  306.6 6.5 %far_values.17.refs_0_.refs_1_.refs_4_ = bf16[1024,256]{1,0:T(8,128)(2,1)} custom-call(s32[10,128]{1,0:T(8,128)S(1)} %get-tuple-element.75.lists.refs_0_, s32[24,128]{1,0:T(8,128)S(1)} %get-tuple-element.76.table, bf16[768,256]{1,0:T(8,128)(2,1)} %branch_1_fun.36.after, bf16[1024,3072]{1,0:T(8,128)(2,1)} %get-tuple-element.89.after.p, ...), custom_call_target="tpu_custom_call" | custom-call | tf_op jit(solution)/shard_map/cond/branch_1_fun/far_values/pallas_call | solution.py:604
  316.3 6.6 %far_values.18.refs_0_.refs_1_.refs_8_ = bf16[1024,256]{1,0:T(8,128)(2,1)} custom-call(s32[10,128]{1,0:T(8,128)S(1)} %get-tuple-element.75.lists.refs_0_, s32[24,128]{1,0:T(8,128)S(1)} %get-tuple-element.76.table, bf16[768,256]{1,0:T(8,128)(2,1)} %branch_1_fun.37.after, bf16[1024,3072]{1,0:T(8,128)(2,1)} %get-tuple-element.89.after.p, ...), custom_call_target="tpu_custom_call" | custom-call | tf_op jit(solution)/shard_map/cond/branch_1_fun/far_values/pallas_call | solution.py:604
  324.8 6.4 %far_values.19.refs_0_.refs_1_.refs_12_ = bf16[1024,256]{1,0:T(8,128)(2,1)} custom-call(s32[10,128]{1,0:T(8,128)S(1)} %get-tuple-element.75.lists.refs_0_, s32[24,128]{1,0:T(8,128)S(1)} %get-tuple-element.76.table, bf16[768,256]{1,0:T(8,128)(2,1)} %branch_1_fun.38.after, bf16[1024,3072]{1,0:T(8,128)(2,1)} %get-tuple-element.89.after.p, ...), custom_call_target="tpu_custom_call" | custom-call | tf_op jit(solution)/shard_map/cond/branch_1_fun/far_values/pallas_call | solution.py:604
  333.2 14.9 %collective-permute-done.48.refs_2_.refs_1_ = bf16[768,256]{1,0:T(8,128)(2,1)S(1)} collective-permute-done((bf16[768,256]{1,0:T(8,128)(2,1)}, bf16[768,256]{1,0:T(8,128)(2,1)S(1)}, u32[]{:S(2)}, u32[]{:S(2)}) %collective-permute-start.48) | collective-permute-done | bytes 393248 | tf_op jit(solution)/shard_map/cond/branch_1_fun/ppermute | solution.py:657
  361.0 14.9 %collective-permute-done.49.refs_3_.refs_2_ = bf16[896,256]{1,0:T(8,128)(2,1)S(1)} collective-permute-done((bf16[896,256]{1,0:T(8,128)(2,1)}, bf16[896,256]{1,0:T(8,128)(2,1)S(1)}, u32[]{:S(2)}, u32[]{:S(2)}) %collective-permute-start.49) | collective-permute-done | bytes 458784 | tf_op jit(solution)/shard_map/cond/branch_1_fun/ppermute | solution.py:657
  381.9 8.8 %collective-permute-start.55 = (bf16[896,256]{1,0:T(8,128)(2,1)}, bf16[896,256]{1,0:T(8,128)(2,1)S(1)}, u32[]{:S(2)}, u32[]{:S(2)}) collective-permute-start(bf16[896,256]{1,0:T(8,128)(2,1)} %branch_1_fun.43.refs_0_), channel_id=1, source_target_pairs={{0,8},{4,12},{8,0},{12,4},{16,24},{20,28},{24,16},{28,20},{1,9},{5... | collective-permute-start | bytes 1376264 | tf_op jit(solution)/shard_map/cond/branch_1_fun/ppermute | solution.py:657
  422.9 9.7 %collective-permute-done.59.refs_15_ = bf16[896,256]{1,0:T(8,128)(2,1)S(1)} collective-permute-done((bf16[896,256]{1,0:T(8,128)(2,1)}, bf16[896,256]{1,0:T(8,128)(2,1)S(1)}, u32[]{:S(2)}, u32[]{:S(2)}) %collective-permute-start.59) | collective-permute-done | bytes 458784 | tf_op jit(solution)/shard_map/cond/branch_1_fun/ppermute | solution.py:657
  432.6 6.7 %collective-permute-done.57.refs_11_ = bf16[896,256]{1,0:T(8,128)(2,1)S(1)} collective-permute-done((bf16[896,256]{1,0:T(8,128)(2,1)S(1)}, bf16[896,256]{1,0:T(8,128)(2,1)S(1)}, u32[]{:S(2)}, u32[]{:S(2)}) %collective-permute-start.57) | collective-permute-done | bytes 458784 | tf_op jit(solution)/shard_map/cond/branch_1_fun/ppermute | solution.py:657
  (161 shorter events, 191.4 us)
Async XLA Ops:
  25.2 36.8 %collective-permute-start.31 = (bf16[3008,128]{1,0:T(8,128)(2,1)}, bf16[3008,128]{1,0:T(8,128)(2,1)S(1)}, u32[]{:S(2)}, u32[]{:S(2)}) collective-permute-start(bf16[3008,128]{1,0:T(8,128)(2,1)} %branch_1_fun.24.after), channel_id=1, source_target_pairs={{0,16},{4,20},{8,24},{12,28},{16,0},{20,4},{24,8},{28,12},{1,17},{... | collective-permute-start | bytes 2310152 | tf_op jit(solution)/shard_map/cond/branch_1_fun/ppermute | solution.py:657
  62.9 34.0 %collective-permute-start.33 = (bf16[3008,128]{1,0:T(8,128)(2,1)}, bf16[3008,128]{1,0:T(8,128)(2,1)S(1)}, u32[]{:S(2)}, u32[]{:S(2)}) collective-permute-start(bf16[3008,128]{1,0:T(8,128)(2,1)} %hold.16.refs_0_), channel_id=1, source_target_pairs={{0,16},{4,20},{8,24},{12,28},{16,0},{20,4},{24,8},{28,12},{1,17},{... | collective-permute-start | bytes 2310152 | tf_op jit(solution)/shard_map/cond/branch_1_fun/ppermute | solution.py:657
  62.9 29.1 %collective-permute-start.32 = (bf16[256,1024]{1,0:T(8,128)(2,1)S(1)}, bf16[256,1024]{1,0:T(8,128)(2,1)}, u32[]{:S(2)}, u32[]{:S(2)}) collective-permute-start(bf16[256,1024]{1,0:T(8,128)(2,1)S(1)} %copy-done.24), channel_id=1, source_target_pairs={{0,16},{4,20},{1,17},{5,21},{2,18},{6,22},{3,19},{7,23}} | collective-permute-start | bytes 1572872 | tf_op jit(solution)/shard_map/cond/branch_1_fun/ppermute | solution.py:657
  72.7 53.1 %collective-permute-start.34 = (bf16[3712,128]{1,0:T(8,128)(2,1)}, bf16[3712,128]{1,0:T(8,128)(2,1)}, u32[]{:S(2)}, u32[]{:S(2)}) collective-permute-start(bf16[3712,128]{1,0:T(8,128)(2,1)} %branch_1_fun.26.refs_0_), channel_id=1, source_target_pairs={{0,8},{4,12},{8,0},{12,4},{16,24},{20,28},{24,16},{28,20},{1,9},{5... | collective-permute-start | bytes 2850824 | tf_op jit(solution)/shard_map/cond/branch_1_fun/ppermute | solution.py:657
  97.8 54.5 %collective-permute-start.38 = (bf16[3008,128]{1,0:T(8,128)(2,1)}, bf16[3008,128]{1,0:T(8,128)(2,1)S(1)}, u32[]{:S(2)}, u32[]{:S(2)}) collective-permute-start(bf16[3008,128]{1,0:T(8,128)(2,1)} %hold.17.refs_0_), channel_id=1, source_target_pairs={{0,16},{4,20},{8,24},{12,28},{16,0},{20,4},{24,8},{28,12},{1,17},{... | collective-permute-start | bytes 2310152 | tf_op jit(solution)/shard_map/cond/branch_1_fun/ppermute | solution.py:657
  98.4 41.8 %collective-permute-start.35 = (bf16[256,1024]{1,0:T(8,128)(2,1)}, bf16[256,1024]{1,0:T(8,128)(2,1)}, u32[]{:S(2)}, u32[]{:S(2)}) collective-permute-start(bf16[256,1024]{1,0:T(8,128)(2,1)} %either.21.after.a), channel_id=1, source_target_pairs={{0,8},{4,12},{16,24},{20,28},{1,9},{5,13},{17,25},{21,29},{2,10},{... | collective-permute-start | bytes 1572872 | tf_op jit(solution)/shard_map/cond/branch_1_fun/ppermute | solution.py:657
  114.8 27.4 %collective-permute-start.36 = (bf16[128,2048]{1,0:T(8,128)(2,1)}, bf16[128,2048]{1,0:T(8,128)(2,1)}, u32[]{:S(2)}, u32[]{:S(2)}) collective-permute-start(bf16[128,2048]{1,0:T(8,128)(2,1)} %get-tuple-element.85), channel_id=1, source_target_pairs={{4,0},{8,4},{12,8},{16,12},{20,16},{24,20},{28,24},{5,1},{9,5},{13... | collective-permute-start | bytes 1572872 | tf_op jit(solution)/shard_map/cond/branch_1_fun/ppermute | solution.py:657
  118.2 33.3 %collective-permute-start.37 = (bf16[128,2048]{1,0:T(8,128)(2,1)}, bf16[128,2048]{1,0:T(8,128)(2,1)S(1)}, u32[]{:S(2)}, u32[]{:S(2)}) collective-permute-start(bf16[128,2048]{1,0:T(8,128)(2,1)} %get-tuple-element.80.refs_0_), channel_id=1, source_target_pairs={{0,4},{4,8},{8,12},{12,16},{16,20},{20,24},{24,28},{1,5},{5,9},{9,... | collective-permute-start | bytes 1572872 | tf_op jit(solution)/shard_map/cond/branch_1_fun/ppermute | solution.py:657
  125.8 46.0 %collective-permute-start.39 = (bf16[3712,128]{1,0:T(8,128)(2,1)}, bf16[3712,128]{1,0:T(8,128)(2,1)}, u32[]{:S(2)}, u32[]{:S(2)}) collective-permute-start(bf16[3712,128]{1,0:T(8,128)(2,1)} %branch_1_fun.28.refs_0_), channel_id=1, source_target_pairs={{0,8},{4,12},{8,0},{12,4},{16,24},{20,28},{24,16},{28,20},{1,9},{5... | collective-permute-start | bytes 2850824 | tf_op jit(solution)/shard_map/cond/branch_1_fun/ppermute | solution.py:657
  153.2 36.1 %collective-permute-start.41 = (bf16[3008,128]{1,0:T(8,128)(2,1)}, bf16[3008,128]{1,0:T(8,128)(2,1)S(1)}, u32[]{:S(2)}, u32[]{:S(2)}) collective-permute-start(bf16[3008,128]{1,0:T(8,128)(2,1)} %hold.19.refs_0_), channel_id=1, source_target_pairs={{0,16},{4,20},{8,24},{12,28},{16,0},{20,4},{24,8},{28,12},{1,17},{... | collective-permute-start | bytes 2310152 | tf_op jit(solution)/shard_map/cond/branch_1_fun/ppermute | solution.py:657
  154.1 22.9 %collective-permute-start.40 = (bf16[256,1024]{1,0:T(8,128)(2,1)S(1)}, bf16[256,1024]{1,0:T(8,128)(2,1)}, u32[]{:S(2)}, u32[]{:S(2)}) collective-permute-start(bf16[256,1024]{1,0:T(8,128)(2,1)S(1)} %copy-done.22), channel_id=1, source_target_pairs={{0,4},{4,0},{8,12},{12,8},{16,20},{20,16},{24,28},{28,24},{1,5},{5... | collective-permute-start | bytes 1572872 | tf_op jit(solution)/shard_map/cond/branch_1_fun/ppermute | solution.py:657
  164.1 45.3 %collective-permute-start.42 = (bf16[3712,128]{1,0:T(8,128)(2,1)}, bf16[3712,128]{1,0:T(8,128)(2,1)}, u32[]{:S(2)}, u32[]{:S(2)}) collective-permute-start(bf16[3712,128]{1,0:T(8,128)(2,1)} %branch_1_fun.31.refs_0_), channel_id=1, source_target_pairs={{0,8},{4,12},{8,0},{12,4},{16,24},{20,28},{24,16},{28,20},{1,9},{5... | collective-permute-start | bytes 2850824 | tf_op jit(solution)/shard_map/cond/branch_1_fun/ppermute | solution.py:657
  193.8 34.6 %collective-permute-start.43 = (bf16[3712,128]{1,0:T(8,128)(2,1)}, bf16[3712,128]{1,0:T(8,128)(2,1)S(1)}, u32[]{:S(2)}, u32[]{:S(2)}) collective-permute-start(bf16[3712,128]{1,0:T(8,128)(2,1)} %branch_1_fun.33.after), channel_id=1, source_target_pairs={{0,8},{4,12},{8,0},{12,4},{16,24},{20,28},{24,16},{28,20},{1,9},{5... | collective-permute-start | bytes 2850824 | tf_op jit(solution)/shard_map/cond/branch_1_fun/ppermute | solution.py:657
  199.1 34.7 %collective-permute-start.44 = (bf16[4352,128]{1,0:T(8,128)(2,1)}, bf16[4352,128]{1,0:T(8,128)(2,1)}, u32[]{:S(2)}, u32[]{:S(2)}) collective-permute-start(bf16[4352,128]{1,0:T(8,128)(2,1)} %branch_1_fun.30.after), channel_id=1, source_target_pairs={{0,4},{4,0},{8,12},{12,8},{16,20},{20,16},{24,28},{28,24},{1,5},{5... | collective-permute-start | bytes 3342344 | tf_op jit(solution)/shard_map/cond/branch_1_fun/ppermute | solution.py:657
  199.2 51.6 %collective-permute-start.45 = (bf16[4352,128]{1,0:T(8,128)(2,1)}, bf16[4352,128]{1,0:T(8,128)(2,1)}, u32[]{:S(2)}, u32[]{:S(2)}) collective-permute-start(bf16[4352,128]{1,0:T(8,128)(2,1)} %branch_1_fun.32.after), channel_id=1, source_target_pairs={{0,4},{4,0},{8,12},{12,8},{16,20},{20,16},{24,28},{28,24},{1,5},{5... | collective-permute-start | bytes 3342344 | tf_op jit(solution)/shard_map/cond/branch_1_fun/ppermute | solution.py:657
  214.0 60.7 %collective-permute-start.46 = (bf16[4352,128]{1,0:T(8,128)(2,1)}, bf16[4352,128]{1,0:T(8,128)(2,1)}, u32[]{:S(2)}, u32[]{:S(2)}) collective-permute-start(bf16[4352,128]{1,0:T(8,128)(2,1)} %branch_1_fun.34.refs_0_), channel_id=1, source_target_pairs={{0,4},{4,0},{8,12},{12,8},{16,20},{20,16},{24,28},{28,24},{1,5},{5... | collective-permute-start | bytes 3342344 | tf_op jit(solution)/shard_map/cond/branch_1_fun/ppermute | solution.py:657
  233.9 62.0 %collective-permute-start.47 = (bf16[4352,128]{1,0:T(8,128)(2,1)}, bf16[4352,128]{1,0:T(8,128)(2,1)S(1)}, u32[]{:S(2)}, u32[]{:S(2)}) collective-permute-start(bf16[4352,128]{1,0:T(8,128)(2,1)} %branch_1_fun.35.after), channel_id=1, source_target_pairs={{0,4},{4,0},{8,12},{12,8},{16,20},{20,16},{24,28},{28,24},{1,5},{5... | collective-permute-start | bytes 3342344 | tf_op jit(solution)/shard_map/cond/branch_1_fun/ppermute | solution.py:657
  305.3 42.8 %collective-permute-start.48 = (bf16[768,256]{1,0:T(8,128)(2,1)}, bf16[768,256]{1,0:T(8,128)(2,1)S(1)}, u32[]{:S(2)}, u32[]{:S(2)}) collective-permute-start(bf16[768,256]{1,0:T(8,128)(2,1)} %branch_1_fun.36.after), channel_id=1, source_target_pairs={{16,0},{20,4},{24,8},{28,12},{17,1},{21,5},{25,9},{29,13},{18,2},{... | collective-permute-start | bytes 1179656 | tf_op jit(solution)/shard_map/cond/branch_1_fun/ppermute | solution.py:657
  315.1 40.5 %collective-permute-start.50 = (bf16[768,256]{1,0:T(8,128)(2,1)}, bf16[768,256]{1,0:T(8,128)(2,1)S(1)}, u32[]{:S(2)}, u32[]{:S(2)}) collective-permute-start(bf16[768,256]{1,0:T(8,128)(2,1)} %branch_1_fun.37.after), channel_id=1, source_target_pairs={{16,0},{20,4},{24,8},{28,12},{17,1},{21,5},{25,9},{29,13},{18,2},{... | collective-permute-start | bytes 1179656 | tf_op jit(solution)/shard_map/cond/branch_1_fun/ppermute | solution.py:657
  350.9 25.0 %collective-permute-start.49 = (bf16[896,256]{1,0:T(8,128)(2,1)}, bf16[896,256]{1,0:T(8,128)(2,1)S(1)}, u32[]{:S(2)}, u32[]{:S(2)}) collective-permute-start(bf16[896,256]{1,0:T(8,128)(2,1)} %branch_1_fun.40.refs_0_), channel_id=1, source_target_pairs={{0,8},{4,12},{8,0},{12,4},{16,24},{20,28},{24,16},{28,20},{1,9},{5... | collective-permute-start | bytes 1376264 | tf_op jit(solution)/shard_map/cond/branch_1_fun/ppermute | solution.py:657
  358.4 32.3 %collective-permute-start.52 = (bf16[896,256]{1,0:T(8,128)(2,1)}, bf16[896,256]{1,0:T(8,128)(2,1)S(1)}, u32[]{:S(2)}, u32[]{:S(2)}) collective-permute-start(bf16[896,256]{1,0:T(8,128)(2,1)} %branch_1_fun.41.refs_0_), channel_id=1, source_target_pairs={{0,8},{4,12},{8,0},{12,4},{16,24},{20,28},{24,16},{28,20},{1,9},{5... | collective-permute-start | bytes 1376264 | tf_op jit(solution)/shard_map/cond/branch_1_fun/ppermute | solution.py:657
  359.7 36.9 %collective-permute-start.56 = (bf16[768,256]{1,0:T(8,128)(2,1)S(1)}, bf16[768,256]{1,0:T(8,128)(2,1)S(1)}, u32[]{:S(2)}, u32[]{:S(2)}) collective-permute-start(bf16[768,256]{1,0:T(8,128)(2,1)S(1)} %copy-done.53), channel_id=1, source_target_pairs={{16,0},{20,4},{24,8},{28,12},{17,1},{21,5},{25,9},{29,13},{18,2},{... | collective-permute-start | bytes 1179656 | tf_op jit(solution)/shard_map/cond/branch_1_fun/ppermute | solution.py:657
  381.9 22.3 %collective-permute-start.55 = (bf16[896,256]{1,0:T(8,128)(2,1)}, bf16[896,256]{1,0:T(8,128)(2,1)S(1)}, u32[]{:S(2)}, u32[]{:S(2)}) collective-permute-start(bf16[896,256]{1,0:T(8,128)(2,1)} %branch_1_fun.43.refs_0_), channel_id=1, source_target_pairs={{0,8},{4,12},{8,0},{12,4},{16,24},{20,28},{24,16},{28,20},{1,9},{5... | collective-permute-start | bytes 1376264 | tf_op jit(solution)/shard_map/cond/branch_1_fun/ppermute | solution.py:657
  415.6 23.7 %collective-permute-start.57 = (bf16[896,256]{1,0:T(8,128)(2,1)S(1)}, bf16[896,256]{1,0:T(8,128)(2,1)S(1)}, u32[]{:S(2)}, u32[]{:S(2)}) collective-permute-start(bf16[896,256]{1,0:T(8,128)(2,1)S(1)} %copy-done.48), channel_id=1, source_target_pairs={{0,4},{4,0},{8,12},{12,8},{16,20},{20,16},{24,28},{28,24},{1,5},{5... | collective-permute-start | bytes 1376264 | tf_op jit(solution)/shard_map/cond/branch_1_fun/ppermute | solution.py:657
  (36 other events, 283.8 us)

commit v2 on v1

--- a/solution.py
+++ b/solution.py
@@ -17,10 +17,11 @@
 
 neg_big = -1e30
 
-ROUTE_SHARES = ((0.66, 0.545, 0.61), (0.73, 0.6, 0.7), (1.0, 1.0, 1.0))
-PACK_SHARES = ((0.7, 0.35, 0.75), (0.8, 0.45, 0.85), (1.0, 1.0, 1.0))
-PARTS = 2
+ROUTE_SHARES = ((0.65, 0.56, 0.645), (0.71, 0.6, 0.705), (1.0, 1.0, 1.0))
+PACK_SHARES = ((0.7, 0.35, 0.75), (0.85, 0.42, 0.75), (1.0, 1.0, 1.0))
+CHUNKS = ((0, 0, 64), (0, 64, 64), (1, 0, 48), (1, 48, 48), (1, 96, 32))
 UNROLL = 4
+PAIR = 2
 SPLIT = (2, 4, 6)
 
 
@@ -316,11 +317,11 @@
     )(after, before, x)
 
 
-def tile_part(heads_bits, part, rows):
+def tile_part(heads_bits, first, rows):
     def read(own, code):
         head = jnp.right_shift(code, heads_bits)
         pos = code & ((1 << heads_bits) - 1)
-        at = pl.multiple_of(pos * B + part * rows, rows)
+        at = pl.multiple_of(pos * B + first, 16)
         return own[pl.ds(at, rows), pl.ds(pl.multiple_of(head * DH, DH), DH)]
 
     return read
@@ -412,13 +413,16 @@
             copies.append(copy)
 
 
-def start_far(plan, sizes, chunks, pool, sem, copies):
-    rows = B // PARTS
-    for part in range(PARTS):
+def parts_of(which):
+    return [(first, rows) for kind, first, rows in CHUNKS if kind == which]
+
+
+def start_far(plan, sizes, which, chunks, pool, sem, copies):
+    for part, (first, rows) in enumerate(parts_of(which)):
         for s in range(plan.bits):
             copy = pltpu.make_async_copy(
                 chunks[part * plan.bits + s],
-                pool.at[pl.ds(plan.base[s], sizes[s]), pl.ds(part * rows, rows), :],
+                pool.at[pl.ds(plan.base[s], sizes[s]), pl.ds(first, rows), :],
                 sem.at[len(copies)],
             )
             copy.start()
@@ -459,20 +463,25 @@
         col = lax.broadcasted_iota(jnp.int32, (B, win), 1)
         dead = (first & (col < B)) | (last & (col >= 2 * B))
         rows = pl.ds(pl.multiple_of(i * B, B), B)
-        for number, h in enumerate(heads):
-            qt = q[rows, h * DH : (h + 1) * DH]
-            spans = (
-                pl.ds(pl.multiple_of((h * per + i) * B, B), win),
-                pl.ds((h * per + 2 + blk) * B, G * B),
-            )
-            scores = [scores_of(qt, kp[span, :]) for span in spans]
-            scores[0] = jnp.where(dead, neg_big, scores[0])
-            top = peak(scores)
-            total, acc = gather_parts(scores, [vp[span, :] for span in spans], top)
-            acc_out[rows, number * DH : (number + 1) * DH] = acc
-            stat_out[rows, h : h + 1] = top
-            stat_out[rows, hd + h : hd + h + 1] = total
-        return carry
+
+        def some_heads(g, carry):
+            for n in range(PAIR):
+                number = g * PAIR + n
+                h = heads[0] + number
+                qt = q[rows, pl.ds(pl.multiple_of(h * DH, DH), DH)]
+                spans = (
+                    pl.ds(pl.multiple_of((h * per + i) * B, B), win),
+                    pl.ds(pl.multiple_of((h * per + 2 + blk) * B, B), G * B),
+                )
+                scores = [scores_of(qt, kp[span, :]) for span in spans]
+                scores[0] = jnp.where(dead, neg_big, scores[0])
+                top = peak(scores)
+                total, acc = gather_parts(scores, [vp[span, :] for span in spans], top)
+                acc_out[rows, pl.ds(pl.multiple_of(number * DH, DH), DH)] = acc
+                put_stats(stat_out, rows, hd, h, top, total)
+            return carry
+
+        return lax.fori_loop(0, len(heads) // PAIR, some_heads, carry)
 
     lax.fori_loop(0, lists[row + 3, 0], step, 0)
 
@@ -497,11 +506,11 @@
 
 
 def far_scores_body(plan, sizes, lists, table, after, q, k, low, high, shared, *refs):
-    count = PARTS * plan.bits
+    count = len(parts_of(0)) * plan.bits
     chunks, (p_out, stat_out), (near, far, sem) = refs[:count], refs[count : count + 2], refs[count + 2 :]
     hd = plan.heads
     copies = []
-    start_far(plan, sizes, chunks, far, sem, copies)
+    start_far(plan, sizes, 0, chunks, far, sem, copies)
     start_near(plan, range(hd), k, low, high, shared, 0, near, sem, copies)
     for copy in copies:
         copy.wait()
@@ -538,7 +547,7 @@
     return [
         pltpu.VMEM((plan.heads * plan.per_head * B, DH), jnp.bfloat16),
         pltpu.VMEM((sum(plan.full), B, DH), jnp.bfloat16),
-        pltpu.SemaphoreType.DMA((4 * plan.heads + PARTS * plan.bits,)),
+        pltpu.SemaphoreType.DMA((4 * plan.heads + len(CHUNKS) * plan.bits,)),
     ]
 
 
@@ -558,11 +567,11 @@
 
 def far_values_body(plan, sizes, heads, lists, table, after, p, pstat, acc_in, stat, v, low, high,
                     shared, *refs):
-    count = PARTS * plan.bits
+    count = len(parts_of(1)) * plan.bits
     chunks, out, (near, far, sem) = refs[:count], refs[count], refs[count + 1 :]
     hd = plan.heads
     copies = []
-    start_far(plan, sizes, chunks, far, sem, copies)
+    start_far(plan, sizes, 1, chunks, far, sem, copies)
     start_near(plan, heads, v, low, high, shared, 1, near, sem, copies)
     for copy in copies:
         copy.wait()
@@ -636,7 +645,6 @@
     lists, table = make_lists(plan, scal, everyone, ids)
 
     blk_bits = log2(blk_dev)
-    rows = B // PARTS
     row = 2 * bits
     cuts = [0] + [cut for cut in SPLIT if cut < head_dev] + [head_dev]
     teams = [range(low, high) for low, high in zip(cuts, cuts[1:])]
@@ -645,7 +653,7 @@
 
     def branch(sizes, csizes):
         def steps(queries, keys, values, lists, table, scal, odd):
-            got = [[] for _ in range(2 * PARTS)]
+            got = [[] for _ in CHUNKS]
             last = [lists]
 
             def run_after(fn, *args):
@@ -660,11 +668,11 @@
                 return hop(x, [(i, i ^ bit) for i in range(count) if not down_only or i & bit])
 
             def packed_tiles(s, chunk):
-                which, part = chunk // PARTS, chunk % PARTS
+                which, first, rows = CHUNKS[chunk]
                 bases = [plan.own + at for at in plan.base[: s + 1]]
                 return run_after(
                     lambda after: pack(
-                        s, sizes[s], bases, tile_part(blk_bits, part, rows), rows, lists, after,
+                        s, sizes[s], bases, tile_part(blk_bits, first, rows), rows, lists, after,
                         [(keys, values)[which]] + got[chunk], DH,
                     )
                 )
@@ -675,8 +683,9 @@
             def tiles(which):
                 return [
                     x.reshape(-1, rows, DH)
-                    for part in range(PARTS)
-                    for x in got[which * PARTS + part]
+                    for (kind, first, rows), stages in zip(CHUNKS, got)
+                    if kind == which
+                    for x in stages
                 ]
 
             def begin(chunk, packed):
@@ -696,8 +705,7 @@
                 spreads.append(
                     (bit, [(i + j, i + j + bit) for i in range(0, count, 2 * bit) for j in (0, 1)])
                 )
-            chunks = 2 * PARTS
-            last_spread = max(len(spreads), chunks - 2)
+            chunks = len(CHUNKS)
             nears = []
 
             def near_half(number):
@@ -709,7 +717,7 @@
                     )
                 )
 
-            for step in range(chunks + bits - 1):
+            for step in range(max(chunks + bits - 1, len(spreads) + 2)):
                 there = None
                 if step < len(spreads):
                     bit, pairs = spreads[step]
@@ -719,8 +727,6 @@
                 if step + 1 < chunks:
                     begin(step + 1, coming)
                 for s in range(1, bits):
-                    if s == 2 and step == max(chunks - 1, len(spreads) + 1):
-                        nears.append(near_half(1))
                     if 0 <= step + 1 - s < chunks:
                         stage(s, step + 1 - s)
                     if s == 1 and step + 2 < chunks:
@@ -732,17 +738,14 @@
                     shared_values = run_after(either, odd, there, held)
                 if step == 1:
                     low = run_after(hold, high, low)
-                if step == last_spread:
-                    nears.append(near_half(0))
-                if step == max(chunks, last_spread):
-                    p, pstat = run_after(
-                        lambda after: far_scores(
-                            plan, sizes, lists, table, after, queries, keys, low, high,
-                            shared_keys, tiles(0),
-                        )
-                    )
-            if len(nears) == 1:
-                nears.append(near_half(1))
+                if step in (len(spreads), len(spreads) + 1):
+                    nears.append(near_half(step - len(spreads)))
+            p, pstat = run_after(
+                lambda after: far_scores(
+                    plan, sizes, lists, table, after, queries, keys, low, high, shared_keys,
+                    tiles(0),
+                )
+            )
 
             sources = []
 
@@ -756,20 +759,21 @@
                 )
                 held.append(swap(packed, count >> (s + 1), count, s == 0))
 
-            for half, heads in enumerate(teams):
-                acc, stat = nears[heads[0] // (head_dev // 2)]
-                attended = run_after(
-                    lambda after: far_values(
-                        plan, sizes, heads, lists, table, after, p, pstat, acc, stat, values,
-                        low, high, shared_values, tiles(1),
+            for step in range(len(teams) + 2 * (bits - 1)):
+                if step < len(teams):
+                    heads = teams[step]
+                    acc, stat = nears[heads[0] // (head_dev // 2)]
+                    attended = run_after(
+                        lambda after: far_values(
+                            plan, sizes, heads, lists, table, after, p, pstat, acc, stat, values,
+                            low, high, shared_values, tiles(1),
+                        )
                     )
-                )
-                sources.append([attended])
-                pack_stage(0, sources[half])
-            for step in range(len(teams) + bits - 2):
-                for s in range(1, bits):
-                    if 0 <= step + 1 - s < len(teams):
-                        pack_stage(s, sources[step + 1 - s])
+                    sources.append([attended])
+                    pack_stage(0, sources[step])
+                for s in reversed(range(1, bits)):
+                    if 0 <= step - 2 * s < len(teams):
+                        pack_stage(s, sources[step - 2 * s])
             bases = [plan.blk + at for at in plan.cbase + [sum(plan.cfull)]]
             widths = [len(heads) * DH for heads in teams]
             return final(row, blk_dev, bases, lists, sum(sources, []), widths)

time: 449 us -> 451 us (level)
  Pallas kernels: 146 us -> 154 us
    pallas_call x24 -> x27, Pallas kernels: 72.6 us -> 80.6 us  [pack(): pl.pallas_call(functools.partial(pack_body, row, size, bases, own_part, r...]
    ppermute x30 -> x33, starting transfers between devices: 67.1 us -> 63 us  [hop(): return lax.ppermute(x, 'seq', pairs)]
    ppermute x30 -> x33, waiting for transfers between devices: 197 us -> 195 us  [hop(): return lax.ppermute(x, 'seq', pairs)]
    cond x54 -> x58, local copies, waits for them, and re-layouts: 14.2 us -> 13.4 us
  transfers between devices with their start and end apart: 31 -> 34, of which waited for: 21 -> 19; matrix products, arithmetic and copies ran while one was open for 0% -> 0% of each run, Pallas kernels for 29% -> 30%
where the time goes in v2:
time: 451 us; the launch traced here: 448 us
  waiting for transfers between devices  201 us (45%)
  Pallas kernels  154 us (34%)
  starting transfers between devices  69.1 us (15%)
  local copies, waits for them, and re-layouts  18.3 us (4%)
    ppermute x33, waiting for transfers between devices, hop(): return lax.ppermute(x, 'seq', pairs)  195 us
    pallas_call x27, Pallas kernels, pack(): pl.pallas_call(functools.partial(pack_body, row, size, bases, own_part, r...  80.6 us
    ppermute x33, starting transfers between devices, hop(): return lax.ppermute(x, 'seq', pairs)  63 us
    pallas_call x4, Pallas kernels, far_values(): pl.pallas_call(functools.partial(far_values_body, plan, sizes, heads), ou...  26 us
    pallas_call x2, Pallas kernels, near_attend(): pl.pallas_call(functools.partial(near_body, plan, heads), out_shape=(jax....  17 us
    cond x58, local copies, waits for them, and re-layouts  13.4 us
    pallas_call x1, Pallas kernels, far_scores(): pl.pallas_call(functools.partial(far_scores_body, plan, sizes), out_shape...  11.4 us
    pallas_call x5, Pallas kernels, either(): pl.pallas_call(either_body, out_shape=jax.ShapeDtypeStruct(a.shape, a.dty...  10.3 us
  transfers between devices with their start and end apart: 34, of which 19 were waited for; matrix products, arithmetic and copies ran while one was open for 0% of the time, Pallas kernels for 30%

profile of v2, /device:TPU:2, one launch (start us, length us, event | category | flops | bytes accessed | tf_op | source)
XLA Modules:
  0.0 447.6 jit_solution(947523843104242623)
XLA Ops:
  3.3 6.1 %all-to-all-start = ((s32[32,1,256]{2,1,0:T(1,128)}), s32[32,1,256]{2,1,0:T(1,128)S(1)}, u32[]{:S(2)}, u32[]{:S(2)}) async-start(s32[32,1,256]{2,1,0:T(1,128)} %reshape.202), calls=%async_computation | async-start | bytes 65536 | tf_op jit(solution)/shard_map/all_to_all | solution.py:640
  21.4 424.8 %conditional.1 = (bf16[1024,1024]{1,0:T(8,128)(2,1)S(1)}) conditional(s32[]{:T(128)} %bitcast.56, (s32[10,128]{1,0:T(8,128)S(1)}, bf16[1024,1024]{1,0:T(8,128)(2,1)}, bf16[1024,1024]{1,0:T(8,128)(2,1)}, s32[3]{0:T(128)S(1)}, s32[]{:T(128)}, /*index=5*/s32[2]{0:T(128)S(1)}, bf16[1024,1024]{1,0:T(8,128)(2,1)}, ...), branch_computations={%region_0.1_spmd, %region_1.2_spmd, %region_2.3_spmd} | conditional | flops 12 | bytes 175376320 | solution.py:783
  33.5 11.0 %collective-permute-done.33.b = bf16[256,1024]{1,0:T(8,128)(2,1)S(1)} collective-permute-done((bf16[256,1024]{1,0:T(8,128)(2,1)}, bf16[256,1024]{1,0:T(8,128)(2,1)S(1)}, u32[]{:S(2)}, u32[]{:S(2)}) %collective-permute-start.33) | collective-permute-done | bytes 524320 | tf_op jit(solution)/shard_map/cond/branch_1_fun/ppermute | solution.py:665
  47.4 13.9 %collective-permute-done.34.before.refs_2_ = bf16[2944,128]{1,0:T(8,128)(2,1)S(1)} collective-permute-done((bf16[2944,128]{1,0:T(8,128)(2,1)}, bf16[2944,128]{1,0:T(8,128)(2,1)S(1)}, u32[]{:S(2)}, u32[]{:S(2)}) %collective-permute-start.34) | collective-permute-done | bytes 753696 | tf_op jit(solution)/shard_map/cond/branch_1_fun/ppermute | solution.py:665
  75.1 39.8 %collective-permute-done.35.b = bf16[256,1024]{1,0:T(8,128)(2,1)} collective-permute-done((bf16[256,1024]{1,0:T(8,128)(2,1)S(1)}, bf16[256,1024]{1,0:T(8,128)(2,1)}, u32[]{:S(2)}, u32[]{:S(2)}) %collective-permute-start.35) | collective-permute-done | bytes 524320 | tf_op jit(solution)/shard_map/cond/branch_1_fun/ppermute | solution.py:665
  147.2 9.2 %collective-permute-done.40.x = bf16[128,2048]{1,0:T(8,128)(2,1)S(1)} collective-permute-done((bf16[128,2048]{1,0:T(8,128)(2,1)}, bf16[128,2048]{1,0:T(8,128)(2,1)S(1)}, u32[]{:S(2)}, u32[]{:S(2)}) %collective-permute-start.40) | collective-permute-done | bytes 524320 | tf_op jit(solution)/shard_map/cond/branch_1_fun/ppermute | solution.py:665
  166.9 9.9 %collective-permute-done.42.refs_3_ = bf16[3712,128]{1,0:T(8,128)(2,1)} collective-permute-done((bf16[3712,128]{1,0:T(8,128)(2,1)}, bf16[3712,128]{1,0:T(8,128)(2,1)}, u32[]{:S(2)}, u32[]{:S(2)}) %collective-permute-start.42) | collective-permute-done | bytes 950304 | tf_op jit(solution)/shard_map/cond/branch_1_fun/ppermute | solution.py:665
  186.1 8.5 %near_attend.8 = (f32[1024,512]{1,0:T(8,128)}, f32[1024,128]{1,0:T(8,128)}) custom-call(s32[10,128]{1,0:T(8,128)S(1)} %get-tuple-element.75.lists.refs_0_, s32[2]{0:T(128)S(1)} %get-tuple-element.77.scal, bf16[256,1024]{1,0:T(8,128)(2,1)} %either.24.after.refs_5_.shared, bf16[1024,1024]{1,0:T(8,128)(2,1)} %get-tuple-element.132.q, ...), custom_call_target="tpu_custom_call" | custom-call | tf_op jit(solution)/shard_map/cond/branch_1_fun/near_attend/pallas_call | solution.py:491
  204.6 9.7 %collective-permute-start.46 = (bf16[1472,128]{1,0:T(8,128)(2,1)}, bf16[1472,128]{1,0:T(8,128)(2,1)S(1)}, u32[]{:S(2)}, u32[]{:S(2)}) collective-permute-start(bf16[1472,128]{1,0:T(8,128)(2,1)} %hold.24.refs_0_), channel_id=1, source_target_pairs={{0,16},{4,20},{8,24},{12,28},{16,0},{20,4},{24,8},{28,12},{1,17},{... | collective-permute-start | bytes 1130504 | tf_op jit(solution)/shard_map/cond/branch_1_fun/ppermute | solution.py:665
  221.5 8.5 %near_attend.9 = (f32[1024,512]{1,0:T(8,128)}, f32[1024,128]{1,0:T(8,128)}) custom-call(s32[10,128]{1,0:T(8,128)S(1)} %get-tuple-element.75.lists.refs_0_, s32[2]{0:T(128)S(1)} %get-tuple-element.77.scal, bf16[3264,128]{1,0:T(8,128)(2,1)} %branch_1_fun.38.after, bf16[1024,1024]{1,0:T(8,128)(2,1)} %get-tuple-element.132.q, ...), custom_call_target="tpu_custom_call" | custom-call | tf_op jit(solution)/shard_map/cond/branch_1_fun/near_attend/pallas_call | solution.py:491
  234.1 7.9 %collective-permute-start.48 = (bf16[1856,128]{1,0:T(8,128)(2,1)}, bf16[1856,128]{1,0:T(8,128)(2,1)S(1)}, u32[]{:S(2)}, u32[]{:S(2)}) collective-permute-start(bf16[1856,128]{1,0:T(8,128)(2,1)} %branch_1_fun.39.refs_0_), channel_id=1, source_target_pairs={{0,8},{4,12},{8,0},{12,4},{16,24},{20,28},{24,16},{28,20},{1,9},{5... | collective-permute-start | bytes 1425416 | tf_op jit(solution)/shard_map/cond/branch_1_fun/ppermute | solution.py:665
  256.7 9.3 %collective-permute-done.50 = bf16[4352,128]{1,0:T(8,128)(2,1)} collective-permute-done((bf16[4352,128]{1,0:T(8,128)(2,1)}, bf16[4352,128]{1,0:T(8,128)(2,1)}, u32[]{:S(2)}, u32[]{:S(2)}) %collective-permute-start.50) | collective-permute-done | bytes 1114144 | tf_op jit(solution)/shard_map/cond/branch_1_fun/ppermute | solution.py:665
  265.9 11.4 %far_scores.4 = (bf16[1024,3072]{1,0:T(8,128)(2,1)}, f32[1024,128]{1,0:T(8,128)}) custom-call(s32[10,128]{1,0:T(8,128)S(1)} %get-tuple-element.75.lists.refs_0_, s32[24,128]{1,0:T(8,128)S(1)} %get-tuple-element.76.table, bf16[2176,128]{1,0:T(8,128)(2,1)} %branch_1_fun.41.after, bf16[1024,1024]{1,0:T(8,128)(2,1)} %get-tuple-element.132.q, ...), custom_call_target="tpu_custom_call" | custom-call | tf_op jit(solution)/shard_map/cond/branch_1_fun/far_scores/pallas_call | solution.py:555
  277.3 6.4 %collective-permute-done.51 = bf16[3264,128]{1,0:T(8,128)(2,1)S(1)} collective-permute-done((bf16[3264,128]{1,0:T(8,128)(2,1)}, bf16[3264,128]{1,0:T(8,128)(2,1)S(1)}, u32[]{:S(2)}, u32[]{:S(2)}) %collective-permute-start.51) | collective-permute-done | bytes 835616 | tf_op jit(solution)/shard_map/cond/branch_1_fun/ppermute | solution.py:665
  283.7 27.5 %collective-permute-done.53 = bf16[2176,128]{1,0:T(8,128)(2,1)S(1)} collective-permute-done((bf16[2176,128]{1,0:T(8,128)(2,1)}, bf16[2176,128]{1,0:T(8,128)(2,1)S(1)}, u32[]{:S(2)}, u32[]{:S(2)}) %collective-permute-start.53) | collective-permute-done | bytes 557088 | tf_op jit(solution)/shard_map/cond/branch_1_fun/ppermute | solution.py:665
  312.1 6.5 %far_values.16.refs_0_.refs_1_ = bf16[1024,256]{1,0:T(8,128)(2,1)} custom-call(s32[10,128]{1,0:T(8,128)S(1)} %get-tuple-element.75.lists.refs_0_, s32[24,128]{1,0:T(8,128)S(1)} %get-tuple-element.76.table, bf16[1024,3072]{1,0:T(8,128)(2,1)} %get-tuple-element.89.after.p, bf16[1024,3072]{1,0:T(8,128)(2,1)} %get-tuple-element.89.after.p, ...), custom_call_target="tpu_custom_call" | custom-call | tf_op jit(solution)/shard_map/cond/branch_1_fun/far_values/pallas_call | solution.py:613
  321.8 6.5 %far_values.17.refs_0_.refs_1_.refs_4_ = bf16[1024,256]{1,0:T(8,128)(2,1)} custom-call(s32[10,128]{1,0:T(8,128)S(1)} %get-tuple-element.75.lists.refs_0_, s32[24,128]{1,0:T(8,128)S(1)} %get-tuple-element.76.table, bf16[768,256]{1,0:T(8,128)(2,1)} %branch_1_fun.42.after, bf16[1024,3072]{1,0:T(8,128)(2,1)} %get-tuple-element.89.after.p, ...), custom_call_target="tpu_custom_call" | custom-call | tf_op jit(solution)/shard_map/cond/branch_1_fun/far_values/pallas_call | solution.py:613
  331.6 6.5 %far_values.18.refs_0_.refs_1_.refs_8_ = bf16[1024,256]{1,0:T(8,128)(2,1)} custom-call(s32[10,128]{1,0:T(8,128)S(1)} %get-tuple-element.75.lists.refs_0_, s32[24,128]{1,0:T(8,128)S(1)} %get-tuple-element.76.table, bf16[768,256]{1,0:T(8,128)(2,1)} %branch_1_fun.43.after, bf16[1024,3072]{1,0:T(8,128)(2,1)} %get-tuple-element.89.after.p, ...), custom_call_target="tpu_custom_call" | custom-call | tf_op jit(solution)/shard_map/cond/branch_1_fun/far_values/pallas_call | solution.py:613
  341.3 17.0 %collective-permute-done.54.refs_2_.refs_1_ = bf16[768,256]{1,0:T(8,128)(2,1)S(1)} collective-permute-done((bf16[768,256]{1,0:T(8,128)(2,1)}, bf16[768,256]{1,0:T(8,128)(2,1)S(1)}, u32[]{:S(2)}, u32[]{:S(2)}) %collective-permute-start.54) | collective-permute-done | bytes 393248 | tf_op jit(solution)/shard_map/cond/branch_1_fun/ppermute | solution.py:665
  361.1 6.5 %far_values.19.refs_0_.refs_1_.refs_12_ = bf16[1024,256]{1,0:T(8,128)(2,1)} custom-call(s32[10,128]{1,0:T(8,128)S(1)} %get-tuple-element.75.lists.refs_0_, s32[24,128]{1,0:T(8,128)S(1)} %get-tuple-element.76.table, bf16[768,256]{1,0:T(8,128)(2,1)} %branch_1_fun.45.after, bf16[1024,3072]{1,0:T(8,128)(2,1)} %get-tuple-element.89.after.p, ...), custom_call_target="tpu_custom_call" | custom-call | tf_op jit(solution)/shard_map/cond/branch_1_fun/far_values/pallas_call | solution.py:613
  376.3 10.5 %collective-permute-done.55.refs_3_.refs_2_ = bf16[768,256]{1,0:T(8,128)(2,1)S(1)} collective-permute-done((bf16[768,256]{1,0:T(8,128)(2,1)}, bf16[768,256]{1,0:T(8,128)(2,1)S(1)}, u32[]{:S(2)}, u32[]{:S(2)}) %collective-permute-start.55) | collective-permute-done | bytes 393248 | tf_op jit(solution)/shard_map/cond/branch_1_fun/ppermute | solution.py:665
  392.7 7.1 %collective-permute-done.58.refs_3_.refs_6_ = bf16[768,256]{1,0:T(8,128)(2,1)S(1)} collective-permute-done((bf16[768,256]{1,0:T(8,128)(2,1)}, bf16[768,256]{1,0:T(8,128)(2,1)S(1)}, u32[]{:S(2)}, u32[]{:S(2)}) %collective-permute-start.58) | collective-permute-done | bytes 393248 | tf_op jit(solution)/shard_map/cond/branch_1_fun/ppermute | solution.py:665
  426.0 8.4 %collective-permute-done.65.refs_15_ = bf16[768,256]{1,0:T(8,128)(2,1)S(1)} collective-permute-done((bf16[768,256]{1,0:T(8,128)(2,1)}, bf16[768,256]{1,0:T(8,128)(2,1)S(1)}, u32[]{:S(2)}, u32[]{:S(2)}) %collective-permute-start.65) | collective-permute-done | bytes 393248 | tf_op jit(solution)/shard_map/cond/branch_1_fun/ppermute | solution.py:665
  434.5 7.4 %collective-permute-done.63.refs_11_ = bf16[768,256]{1,0:T(8,128)(2,1)S(1)} collective-permute-done((bf16[768,256]{1,0:T(8,128)(2,1)S(1)}, bf16[768,256]{1,0:T(8,128)(2,1)S(1)}, u32[]{:S(2)}, u32[]{:S(2)}) %collective-permute-start.63) | collective-permute-done | bytes 393248 | tf_op jit(solution)/shard_map/cond/branch_1_fun/ppermute | solution.py:665
  (175 shorter events, 190.6 us)
Async XLA Ops:
  25.2 36.1 %collective-permute-start.34 = (bf16[2944,128]{1,0:T(8,128)(2,1)}, bf16[2944,128]{1,0:T(8,128)(2,1)S(1)}, u32[]{:S(2)}, u32[]{:S(2)}) collective-permute-start(bf16[2944,128]{1,0:T(8,128)(2,1)} %branch_1_fun.27.after), channel_id=1, source_target_pairs={{0,16},{4,20},{8,24},{12,28},{16,0},{20,4},{24,8},{28,12},{1,17},{... | collective-permute-start | bytes 2261000 | tf_op jit(solution)/shard_map/cond/branch_1_fun/ppermute | solution.py:665
  66.4 67.1 %collective-permute-start.37 = (bf16[3712,128]{1,0:T(8,128)(2,1)}, bf16[3712,128]{1,0:T(8,128)(2,1)}, u32[]{:S(2)}, u32[]{:S(2)}) collective-permute-start(bf16[3712,128]{1,0:T(8,128)(2,1)} %branch_1_fun.29.refs_0_), channel_id=1, source_target_pairs={{0,8},{4,12},{8,0},{12,4},{16,24},{20,28},{24,16},{28,20},{1,9},{5... | collective-permute-start | bytes 2850824 | tf_op jit(solution)/shard_map/cond/branch_1_fun/ppermute | solution.py:665
  66.5 50.4 %collective-permute-start.36 = (bf16[2944,128]{1,0:T(8,128)(2,1)S(1)}, bf16[2944,128]{1,0:T(8,128)(2,1)}, u32[]{:S(2)}, u32[]{:S(2)}) collective-permute-start(bf16[2944,128]{1,0:T(8,128)(2,1)S(1)} %copy-done.22), channel_id=1, source_target_pairs={{0,16},{4,20},{8,24},{12,28},{16,0},{20,4},{24,8},{28,12},{1,17},{... | collective-permute-start | bytes 2261000 | tf_op jit(solution)/shard_map/cond/branch_1_fun/ppermute | solution.py:665
  67.7 47.2 %collective-permute-start.35 = (bf16[256,1024]{1,0:T(8,128)(2,1)S(1)}, bf16[256,1024]{1,0:T(8,128)(2,1)}, u32[]{:S(2)}, u32[]{:S(2)}) collective-permute-start(bf16[256,1024]{1,0:T(8,128)(2,1)S(1)} %copy-done.32), channel_id=1, source_target_pairs={{0,16},{4,20},{1,17},{5,21},{2,18},{6,22},{3,19},{7,23}} | collective-permute-start | bytes 1572872 | tf_op jit(solution)/shard_map/cond/branch_1_fun/ppermute | solution.py:665
  116.9 40.3 %collective-permute-start.41 = (bf16[2208,128]{1,0:T(8,128)(2,1)}, bf16[2208,128]{1,0:T(8,128)(2,1)}, u32[]{:S(2)}, u32[]{:S(2)}) collective-permute-start(bf16[2208,128]{1,0:T(8,128)(2,1)} %hold.21.refs_0_), channel_id=1, source_target_pairs={{0,16},{4,20},{8,24},{12,28},{16,0},{20,4},{24,8},{28,12},{1,17},{... | collective-permute-start | bytes 1695752 | tf_op jit(solution)/shard_map/cond/branch_1_fun/ppermute | solution.py:665
  120.4 24.7 %collective-permute-start.38 = (bf16[256,1024]{1,0:T(8,128)(2,1)}, bf16[256,1024]{1,0:T(8,128)(2,1)}, u32[]{:S(2)}, u32[]{:S(2)}) collective-permute-start(bf16[256,1024]{1,0:T(8,128)(2,1)} %either.21.after.a), channel_id=1, source_target_pairs={{0,8},{4,12},{16,24},{20,28},{1,9},{5,13},{17,25},{21,29},{2,10},{... | collective-permute-start | bytes 1572872 | tf_op jit(solution)/shard_map/cond/branch_1_fun/ppermute | solution.py:665
  125.5 30.9 %collective-permute-start.40 = (bf16[128,2048]{1,0:T(8,128)(2,1)}, bf16[128,2048]{1,0:T(8,128)(2,1)S(1)}, u32[]{:S(2)}, u32[]{:S(2)}) collective-permute-start(bf16[128,2048]{1,0:T(8,128)(2,1)} %get-tuple-element.80.refs_0_), channel_id=1, source_target_pairs={{0,4},{4,8},{8,12},{12,16},{16,20},{20,24},{24,28},{1,5},{5,9},{9,... | collective-permute-start | bytes 1572872 | tf_op jit(solution)/shard_map/cond/branch_1_fun/ppermute | solution.py:665
  133.5 43.3 %collective-permute-start.42 = (bf16[3712,128]{1,0:T(8,128)(2,1)}, bf16[3712,128]{1,0:T(8,128)(2,1)}, u32[]{:S(2)}, u32[]{:S(2)}) collective-permute-start(bf16[3712,128]{1,0:T(8,128)(2,1)} %branch_1_fun.31.refs_0_), channel_id=1, source_target_pairs={{0,8},{4,12},{8,0},{12,4},{16,24},{20,28},{24,16},{28,20},{1,9},{5... | collective-permute-start | bytes 2850824 | tf_op jit(solution)/shard_map/cond/branch_1_fun/ppermute | solution.py:665
  157.2 37.4 %collective-permute-start.44 = (bf16[2208,128]{1,0:T(8,128)(2,1)}, bf16[2208,128]{1,0:T(8,128)(2,1)S(1)}, u32[]{:S(2)}, u32[]{:S(2)}) collective-permute-start(bf16[2208,128]{1,0:T(8,128)(2,1)} %hold.23.refs_0_), channel_id=1, source_target_pairs={{0,16},{4,20},{8,24},{12,28},{16,0},{20,4},{24,8},{28,12},{1,17},{... | collective-permute-start | bytes 1695752 | tf_op jit(solution)/shard_map/cond/branch_1_fun/ppermute | solution.py:665
  157.2 24.7 %collective-permute-start.43 = (bf16[256,1024]{1,0:T(8,128)(2,1)}, bf16[256,1024]{1,0:T(8,128)(2,1)}, u32[]{:S(2)}, u32[]{:S(2)}) collective-permute-start(bf16[256,1024]{1,0:T(8,128)(2,1)} %either.22.after.a.b), channel_id=1, source_target_pairs={{0,4},{4,0},{8,12},{12,8},{16,20},{20,16},{24,28},{28,24},{1,5},{5... | collective-permute-start | bytes 1572872 | tf_op jit(solution)/shard_map/cond/branch_1_fun/ppermute | solution.py:665
  160.8 55.5 %collective-permute-start.45 = (bf16[2784,128]{1,0:T(8,128)(2,1)}, bf16[2784,128]{1,0:T(8,128)(2,1)S(1)}, u32[]{:S(2)}, u32[]{:S(2)}) collective-permute-start(bf16[2784,128]{1,0:T(8,128)(2,1)} %branch_1_fun.34.refs_0_), channel_id=1, source_target_pairs={{0,8},{4,12},{8,0},{12,4},{16,24},{20,28},{24,16},{28,20},{1,9},{5... | collective-permute-start | bytes 2138120 | tf_op jit(solution)/shard_map/cond/branch_1_fun/ppermute | solution.py:665
  198.9 43.0 %collective-permute-start.47 = (bf16[2784,128]{1,0:T(8,128)(2,1)}, bf16[2784,128]{1,0:T(8,128)(2,1)}, u32[]{:S(2)}, u32[]{:S(2)}) collective-permute-start(bf16[2784,128]{1,0:T(8,128)(2,1)} %branch_1_fun.37.refs_0_), channel_id=1, source_target_pairs={{0,8},{4,12},{8,0},{12,4},{16,24},{20,28},{24,16},{28,20},{1,9},{5... | collective-permute-start | bytes 2138120 | tf_op jit(solution)/shard_map/cond/branch_1_fun/ppermute | solution.py:665
  204.6 25.4 %collective-permute-start.46 = (bf16[1472,128]{1,0:T(8,128)(2,1)}, bf16[1472,128]{1,0:T(8,128)(2,1)S(1)}, u32[]{:S(2)}, u32[]{:S(2)}) collective-permute-start(bf16[1472,128]{1,0:T(8,128)(2,1)} %hold.24.refs_0_), channel_id=1, source_target_pairs={{0,16},{4,20},{8,24},{12,28},{16,0},{20,4},{24,8},{28,12},{1,17},{... | collective-permute-start | bytes 1130504 | tf_op jit(solution)/shard_map/cond/branch_1_fun/ppermute | solution.py:665
  214.3 42.4 %collective-permute-start.49 = (bf16[4352,128]{1,0:T(8,128)(2,1)}, bf16[4352,128]{1,0:T(8,128)(2,1)}, u32[]{:S(2)}, u32[]{:S(2)}) collective-permute-start(bf16[4352,128]{1,0:T(8,128)(2,1)} %branch_1_fun.33.after), channel_id=1, source_target_pairs={{0,4},{4,0},{8,12},{12,8},{16,20},{20,16},{24,28},{28,24},{1,5},{5... | collective-permute-start | bytes 3342344 | tf_op jit(solution)/shard_map/cond/branch_1_fun/ppermute | solution.py:665
  214.3 51.6 %collective-permute-start.50 = (bf16[4352,128]{1,0:T(8,128)(2,1)}, bf16[4352,128]{1,0:T(8,128)(2,1)}, u32[]{:S(2)}, u32[]{:S(2)}) collective-permute-start(bf16[4352,128]{1,0:T(8,128)(2,1)} %branch_1_fun.36.after), channel_id=1, source_target_pairs={{0,4},{4,0},{8,12},{12,8},{16,20},{20,16},{24,28},{28,24},{1,5},{5... | collective-permute-start | bytes 3342344 | tf_op jit(solution)/shard_map/cond/branch_1_fun/ppermute | solution.py:665
  242.0 41.8 %collective-permute-start.51 = (bf16[3264,128]{1,0:T(8,128)(2,1)}, bf16[3264,128]{1,0:T(8,128)(2,1)S(1)}, u32[]{:S(2)}, u32[]{:S(2)}) collective-permute-start(bf16[3264,128]{1,0:T(8,128)(2,1)} %branch_1_fun.38.after), channel_id=1, source_target_pairs={{0,4},{4,0},{8,12},{12,8},{16,20},{20,16},{24,28},{28,24},{1,5},{5... | collective-permute-start | bytes 2506760 | tf_op jit(solution)/shard_map/cond/branch_1_fun/ppermute | solution.py:665
  246.3 64.9 %collective-permute-start.52 = (bf16[3264,128]{1,0:T(8,128)(2,1)}, bf16[3264,128]{1,0:T(8,128)(2,1)}, u32[]{:S(2)}, u32[]{:S(2)}) collective-permute-start(bf16[3264,128]{1,0:T(8,128)(2,1)} %branch_1_fun.40.refs_0_), channel_id=1, source_target_pairs={{0,4},{4,0},{8,12},{12,8},{16,20},{20,16},{24,28},{28,24},{1,5},{5... | collective-permute-start | bytes 2506760 | tf_op jit(solution)/shard_map/cond/branch_1_fun/ppermute | solution.py:665
  256.7 54.6 %collective-permute-start.53 = (bf16[2176,128]{1,0:T(8,128)(2,1)}, bf16[2176,128]{1,0:T(8,128)(2,1)S(1)}, u32[]{:S(2)}, u32[]{:S(2)}) collective-permute-start(bf16[2176,128]{1,0:T(8,128)(2,1)} %branch_1_fun.41.after), channel_id=1, source_target_pairs={{0,4},{4,0},{8,12},{12,8},{16,20},{20,16},{24,28},{28,24},{1,5},{5... | collective-permute-start | bytes 1671176 | tf_op jit(solution)/shard_map/cond/branch_1_fun/ppermute | solution.py:665
  320.5 37.8 %collective-permute-start.54 = (bf16[768,256]{1,0:T(8,128)(2,1)}, bf16[768,256]{1,0:T(8,128)(2,1)S(1)}, u32[]{:S(2)}, u32[]{:S(2)}) collective-permute-start(bf16[768,256]{1,0:T(8,128)(2,1)} %branch_1_fun.42.after), channel_id=1, source_target_pairs={{16,0},{20,4},{24,8},{28,12},{17,1},{21,5},{25,9},{29,13},{18,2},{... | collective-permute-start | bytes 1179656 | tf_op jit(solution)/shard_map/cond/branch_1_fun/ppermute | solution.py:665
  330.3 39.3 %collective-permute-start.56 = (bf16[768,256]{1,0:T(8,128)(2,1)}, bf16[768,256]{1,0:T(8,128)(2,1)S(1)}, u32[]{:S(2)}, u32[]{:S(2)}) collective-permute-start(bf16[768,256]{1,0:T(8,128)(2,1)} %branch_1_fun.43.after), channel_id=1, source_target_pairs={{16,0},{20,4},{24,8},{28,12},{17,1},{21,5},{25,9},{29,13},{18,2},{... | collective-permute-start | bytes 1179656 | tf_op jit(solution)/shard_map/cond/branch_1_fun/ppermute | solution.py:665
  340.0 49.8 %collective-permute-start.59 = (bf16[768,256]{1,0:T(8,128)(2,1)}, bf16[768,256]{1,0:T(8,128)(2,1)S(1)}, u32[]{:S(2)}, u32[]{:S(2)}) collective-permute-start(bf16[768,256]{1,0:T(8,128)(2,1)} %branch_1_fun.44.refs_0_), channel_id=1, source_target_pairs={{16,0},{20,4},{24,8},{28,12},{17,1},{21,5},{25,9},{29,13},{18,2},{... | collective-permute-start | bytes 1179656 | tf_op jit(solution)/shard_map/cond/branch_1_fun/ppermute | solution.py:665
  361.1 25.7 %collective-permute-start.55 = (bf16[768,256]{1,0:T(8,128)(2,1)}, bf16[768,256]{1,0:T(8,128)(2,1)S(1)}, u32[]{:S(2)}, u32[]{:S(2)}) collective-permute-start(bf16[768,256]{1,0:T(8,128)(2,1)} %branch_1_fun.45.after), channel_id=1, source_target_pairs={{0,8},{4,12},{8,0},{12,4},{16,24},{20,28},{24,16},{28,20},{1,9},{5... | collective-permute-start | bytes 1179656 | tf_op jit(solution)/shard_map/cond/branch_1_fun/ppermute | solution.py:665
  372.4 27.4 %collective-permute-start.58 = (bf16[768,256]{1,0:T(8,128)(2,1)}, bf16[768,256]{1,0:T(8,128)(2,1)S(1)}, u32[]{:S(2)}, u32[]{:S(2)}) collective-permute-start(bf16[768,256]{1,0:T(8,128)(2,1)} %branch_1_fun.47.refs_0_), channel_id=1, source_target_pairs={{0,8},{4,12},{8,0},{12,4},{16,24},{20,28},{24,16},{28,20},{1,9},{5... | collective-permute-start | bytes 1179656 | tf_op jit(solution)/shard_map/cond/branch_1_fun/ppermute | solution.py:665
  375.0 27.8 %collective-permute-start.62 = (bf16[768,256]{1,0:T(8,128)(2,1)S(1)}, bf16[768,256]{1,0:T(8,128)(2,1)S(1)}, u32[]{:S(2)}, u32[]{:S(2)}) collective-permute-start(bf16[768,256]{1,0:T(8,128)(2,1)S(1)} %copy-done.62), channel_id=1, source_target_pairs={{16,0},{20,4},{24,8},{28,12},{17,1},{21,5},{25,9},{29,13},{18,2},{... | collective-permute-start | bytes 1179656 | tf_op jit(solution)/shard_map/cond/branch_1_fun/ppermute | solution.py:665
  (41 other events, 316.6 us)

commit v3 on v2

--- a/solution.py
+++ b/solution.py
@@ -17,11 +17,10 @@
 
 neg_big = -1e30
 
-ROUTE_SHARES = ((0.65, 0.56, 0.645), (0.71, 0.6, 0.705), (1.0, 1.0, 1.0))
+ROUTE_SHARES = ((0.65, 0.555, 0.62), (0.71, 0.6, 0.705), (1.0, 1.0, 1.0))
 PACK_SHARES = ((0.7, 0.35, 0.75), (0.85, 0.42, 0.75), (1.0, 1.0, 1.0))
 CHUNKS = ((0, 0, 64), (0, 64, 64), (1, 0, 48), (1, 48, 48), (1, 96, 32))
 UNROLL = 4
-PAIR = 2
 SPLIT = (2, 4, 6)
 
 
@@ -463,25 +462,20 @@
         col = lax.broadcasted_iota(jnp.int32, (B, win), 1)
         dead = (first & (col < B)) | (last & (col >= 2 * B))
         rows = pl.ds(pl.multiple_of(i * B, B), B)
-
-        def some_heads(g, carry):
-            for n in range(PAIR):
-                number = g * PAIR + n
-                h = heads[0] + number
-                qt = q[rows, pl.ds(pl.multiple_of(h * DH, DH), DH)]
-                spans = (
-                    pl.ds(pl.multiple_of((h * per + i) * B, B), win),
-                    pl.ds(pl.multiple_of((h * per + 2 + blk) * B, B), G * B),
-                )
-                scores = [scores_of(qt, kp[span, :]) for span in spans]
-                scores[0] = jnp.where(dead, neg_big, scores[0])
-                top = peak(scores)
-                total, acc = gather_parts(scores, [vp[span, :] for span in spans], top)
-                acc_out[rows, pl.ds(pl.multiple_of(number * DH, DH), DH)] = acc
-                put_stats(stat_out, rows, hd, h, top, total)
-            return carry
-
-        return lax.fori_loop(0, len(heads) // PAIR, some_heads, carry)
+        for number, h in enumerate(heads):
+            qt = q[rows, h * DH : (h + 1) * DH]
+            spans = (
+                pl.ds(pl.multiple_of((h * per + i) * B, B), win),
+                pl.ds((h * per + 2 + blk) * B, G * B),
+            )
+            scores = [scores_of(qt, kp[span, :]) for span in spans]
+            scores[0] = jnp.where(dead, neg_big, scores[0])
+            top = peak(scores)
+            total, acc = gather_parts(scores, [vp[span, :] for span in spans], top)
+            acc_out[rows, number * DH : (number + 1) * DH] = acc
+            stat_out[rows, h : h + 1] = top
+            stat_out[rows, hd + h : hd + h + 1] = total
+        return carry
 
     lax.fori_loop(0, lists[row + 3, 0], step, 0)
 

time: 451 us -> 450 us (level)
  transfers between devices with their start and end apart: 34 -> 34, of which waited for: 19 -> 19; matrix products, arithmetic and copies ran while one was open for 0% -> 0% of each run, Pallas kernels for 30% -> 29%
where the time goes in v3:
time: 450 us; the launch traced here: 447 us
  waiting for transfers between devices  201 us (45%)
  Pallas kernels  154 us (34%)
  starting transfers between devices  69 us (15%)
  local copies, waits for them, and re-layouts  18.3 us (4%)
    ppermute x33, waiting for transfers between devices, hop(): return lax.ppermute(x, 'seq', pairs)  195 us
    pallas_call x27, Pallas kernels, pack(): pl.pallas_call(functools.partial(pack_body, row, size, bases, own_part, r...  80.6 us
    ppermute x33, starting transfers between devices, hop(): return lax.ppermute(x, 'seq', pairs)  62.8 us
    pallas_call x4, Pallas kernels, far_values(): pl.pallas_call(functools.partial(far_values_body, plan, sizes, heads), ou...  26 us
    pallas_call x2, Pallas kernels, near_attend(): pl.pallas_call(functools.partial(near_body, plan, heads), out_shape=(jax....  16.3 us
    cond x58, local copies, waits for them, and re-layouts  13.4 us
    pallas_call x1, Pallas kernels, far_scores(): pl.pallas_call(functools.partial(far_scores_body, plan, sizes), out_shape...  11.4 us
    pallas_call x5, Pallas kernels, either(): pl.pallas_call(either_body, out_shape=jax.ShapeDtypeStruct(a.shape, a.dty...  10.3 us
  transfers between devices with their start and end apart: 34, of which 19 were waited for; matrix products, arithmetic and copies ran while one was open for 0% of the time, Pallas kernels for 29%

profile of v3, /device:TPU:2, one launch (start us, length us, event | category | flops | bytes accessed | tf_op | source)
XLA Modules:
  0.0 446.7 jit_solution(11904354261484543337)
XLA Ops:
  3.3 6.1 %all-to-all-start = ((s32[32,1,256]{2,1,0:T(1,128)}), s32[32,1,256]{2,1,0:T(1,128)S(1)}, u32[]{:S(2)}, u32[]{:S(2)}) async-start(s32[32,1,256]{2,1,0:T(1,128)} %reshape.202), calls=%async_computation | async-start | bytes 65536 | tf_op jit(solution)/shard_map/all_to_all | solution.py:634
  21.4 423.9 %conditional.1 = (bf16[1024,1024]{1,0:T(8,128)(2,1)S(1)}) conditional(s32[]{:T(128)} %bitcast.56, (s32[10,128]{1,0:T(8,128)S(1)}, bf16[1024,1024]{1,0:T(8,128)(2,1)}, bf16[1024,1024]{1,0:T(8,128)(2,1)}, s32[3]{0:T(128)S(1)}, s32[]{:T(128)}, /*index=5*/s32[2]{0:T(128)S(1)}, bf16[1024,1024]{1,0:T(8,128)(2,1)}, ...), branch_computations={%region_0.1_spmd, %region_1.2_spmd, %region_2.3_spmd} | conditional | flops 12 | bytes 175376320 | solution.py:777
  33.5 11.0 %collective-permute-done.33.b = bf16[256,1024]{1,0:T(8,128)(2,1)S(1)} collective-permute-done((bf16[256,1024]{1,0:T(8,128)(2,1)}, bf16[256,1024]{1,0:T(8,128)(2,1)S(1)}, u32[]{:S(2)}, u32[]{:S(2)}) %collective-permute-start.33) | collective-permute-done | bytes 524320 | tf_op jit(solution)/shard_map/cond/branch_1_fun/ppermute | solution.py:659
  47.4 13.9 %collective-permute-done.34.before.refs_2_ = bf16[2944,128]{1,0:T(8,128)(2,1)S(1)} collective-permute-done((bf16[2944,128]{1,0:T(8,128)(2,1)}, bf16[2944,128]{1,0:T(8,128)(2,1)S(1)}, u32[]{:S(2)}, u32[]{:S(2)}) %collective-permute-start.34) | collective-permute-done | bytes 753696 | tf_op jit(solution)/shard_map/cond/branch_1_fun/ppermute | solution.py:659
  75.1 39.8 %collective-permute-done.35.b = bf16[256,1024]{1,0:T(8,128)(2,1)} collective-permute-done((bf16[256,1024]{1,0:T(8,128)(2,1)S(1)}, bf16[256,1024]{1,0:T(8,128)(2,1)}, u32[]{:S(2)}, u32[]{:S(2)}) %collective-permute-start.35) | collective-permute-done | bytes 524320 | tf_op jit(solution)/shard_map/cond/branch_1_fun/ppermute | solution.py:659
  147.2 9.2 %collective-permute-done.40.x = bf16[128,2048]{1,0:T(8,128)(2,1)S(1)} collective-permute-done((bf16[128,2048]{1,0:T(8,128)(2,1)}, bf16[128,2048]{1,0:T(8,128)(2,1)S(1)}, u32[]{:S(2)}, u32[]{:S(2)}) %collective-permute-start.40) | collective-permute-done | bytes 524320 | tf_op jit(solution)/shard_map/cond/branch_1_fun/ppermute | solution.py:659
  166.9 9.9 %collective-permute-done.42.refs_3_ = bf16[3712,128]{1,0:T(8,128)(2,1)} collective-permute-done((bf16[3712,128]{1,0:T(8,128)(2,1)}, bf16[3712,128]{1,0:T(8,128)(2,1)}, u32[]{:S(2)}, u32[]{:S(2)}) %collective-permute-start.42) | collective-permute-done | bytes 950304 | tf_op jit(solution)/shard_map/cond/branch_1_fun/ppermute | solution.py:659
  186.1 8.2 %near_attend.8 = (f32[1024,512]{1,0:T(8,128)}, f32[1024,128]{1,0:T(8,128)}) custom-call(s32[10,128]{1,0:T(8,128)S(1)} %get-tuple-element.75.lists.refs_0_, s32[2]{0:T(128)S(1)} %get-tuple-element.77.scal, bf16[256,1024]{1,0:T(8,128)(2,1)} %either.24.after.refs_5_.shared, bf16[1024,1024]{1,0:T(8,128)(2,1)} %get-tuple-element.132.q, ...), custom_call_target="tpu_custom_call" | custom-call | tf_op jit(solution)/shard_map/cond/branch_1_fun/near_attend/pallas_call | solution.py:485
  203.9 9.5 %collective-permute-start.46 = (bf16[1472,128]{1,0:T(8,128)(2,1)}, bf16[1472,128]{1,0:T(8,128)(2,1)S(1)}, u32[]{:S(2)}, u32[]{:S(2)}) collective-permute-start(bf16[1472,128]{1,0:T(8,128)(2,1)} %hold.24.refs_0_), channel_id=1, source_target_pairs={{0,16},{4,20},{8,24},{12,28},{16,0},{20,4},{24,8},{28,12},{1,17},{... | collective-permute-start | bytes 1130504 | tf_op jit(solution)/shard_map/cond/branch_1_fun/ppermute | solution.py:659
  220.6 8.2 %near_attend.9 = (f32[1024,512]{1,0:T(8,128)}, f32[1024,128]{1,0:T(8,128)}) custom-call(s32[10,128]{1,0:T(8,128)S(1)} %get-tuple-element.75.lists.refs_0_, s32[2]{0:T(128)S(1)} %get-tuple-element.77.scal, bf16[3264,128]{1,0:T(8,128)(2,1)} %branch_1_fun.38.after, bf16[1024,1024]{1,0:T(8,128)(2,1)} %get-tuple-element.132.q, ...), custom_call_target="tpu_custom_call" | custom-call | tf_op jit(solution)/shard_map/cond/branch_1_fun/near_attend/pallas_call | solution.py:485
  232.8 8.2 %collective-permute-start.48 = (bf16[1856,128]{1,0:T(8,128)(2,1)}, bf16[1856,128]{1,0:T(8,128)(2,1)S(1)}, u32[]{:S(2)}, u32[]{:S(2)}) collective-permute-start(bf16[1856,128]{1,0:T(8,128)(2,1)} %branch_1_fun.39.refs_0_), channel_id=1, source_target_pairs={{0,8},{4,12},{8,0},{12,4},{16,24},{20,28},{24,16},{28,20},{1,9},{5... | collective-permute-start | bytes 1425416 | tf_op jit(solution)/shard_map/cond/branch_1_fun/ppermute | solution.py:659
  255.8 9.3 %collective-permute-done.50 = bf16[4352,128]{1,0:T(8,128)(2,1)} collective-permute-done((bf16[4352,128]{1,0:T(8,128)(2,1)}, bf16[4352,128]{1,0:T(8,128)(2,1)}, u32[]{:S(2)}, u32[]{:S(2)}) %collective-permute-start.50) | collective-permute-done | bytes 1114144 | tf_op jit(solution)/shard_map/cond/branch_1_fun/ppermute | solution.py:659
  265.0 11.4 %far_scores.4 = (bf16[1024,3072]{1,0:T(8,128)(2,1)}, f32[1024,128]{1,0:T(8,128)}) custom-call(s32[10,128]{1,0:T(8,128)S(1)} %get-tuple-element.75.lists.refs_0_, s32[24,128]{1,0:T(8,128)S(1)} %get-tuple-element.76.table, bf16[2176,128]{1,0:T(8,128)(2,1)} %branch_1_fun.41.after, bf16[1024,1024]{1,0:T(8,128)(2,1)} %get-tuple-element.132.q, ...), custom_call_target="tpu_custom_call" | custom-call | tf_op jit(solution)/shard_map/cond/branch_1_fun/far_scores/pallas_call | solution.py:549
  276.4 6.4 %collective-permute-done.51 = bf16[3264,128]{1,0:T(8,128)(2,1)S(1)} collective-permute-done((bf16[3264,128]{1,0:T(8,128)(2,1)}, bf16[3264,128]{1,0:T(8,128)(2,1)S(1)}, u32[]{:S(2)}, u32[]{:S(2)}) %collective-permute-start.51) | collective-permute-done | bytes 835616 | tf_op jit(solution)/shard_map/cond/branch_1_fun/ppermute | solution.py:659
  282.8 27.5 %collective-permute-done.53 = bf16[2176,128]{1,0:T(8,128)(2,1)S(1)} collective-permute-done((bf16[2176,128]{1,0:T(8,128)(2,1)}, bf16[2176,128]{1,0:T(8,128)(2,1)S(1)}, u32[]{:S(2)}, u32[]{:S(2)}) %collective-permute-start.53) | collective-permute-done | bytes 557088 | tf_op jit(solution)/shard_map/cond/branch_1_fun/ppermute | solution.py:659
  311.2 6.5 %far_values.16.refs_0_.refs_1_ = bf16[1024,256]{1,0:T(8,128)(2,1)} custom-call(s32[10,128]{1,0:T(8,128)S(1)} %get-tuple-element.75.lists.refs_0_, s32[24,128]{1,0:T(8,128)S(1)} %get-tuple-element.76.table, bf16[1024,3072]{1,0:T(8,128)(2,1)} %get-tuple-element.89.after.p, bf16[1024,3072]{1,0:T(8,128)(2,1)} %get-tuple-element.89.after.p, ...), custom_call_target="tpu_custom_call" | custom-call | tf_op jit(solution)/shard_map/cond/branch_1_fun/far_values/pallas_call | solution.py:607
  320.9 6.5 %far_values.17.refs_0_.refs_1_.refs_4_ = bf16[1024,256]{1,0:T(8,128)(2,1)} custom-call(s32[10,128]{1,0:T(8,128)S(1)} %get-tuple-element.75.lists.refs_0_, s32[24,128]{1,0:T(8,128)S(1)} %get-tuple-element.76.table, bf16[768,256]{1,0:T(8,128)(2,1)} %branch_1_fun.42.after, bf16[1024,3072]{1,0:T(8,128)(2,1)} %get-tuple-element.89.after.p, ...), custom_call_target="tpu_custom_call" | custom-call | tf_op jit(solution)/shard_map/cond/branch_1_fun/far_values/pallas_call | solution.py:607
  330.7 6.5 %far_values.18.refs_0_.refs_1_.refs_8_ = bf16[1024,256]{1,0:T(8,128)(2,1)} custom-call(s32[10,128]{1,0:T(8,128)S(1)} %get-tuple-element.75.lists.refs_0_, s32[24,128]{1,0:T(8,128)S(1)} %get-tuple-element.76.table, bf16[768,256]{1,0:T(8,128)(2,1)} %branch_1_fun.43.after, bf16[1024,3072]{1,0:T(8,128)(2,1)} %get-tuple-element.89.after.p, ...), custom_call_target="tpu_custom_call" | custom-call | tf_op jit(solution)/shard_map/cond/branch_1_fun/far_values/pallas_call | solution.py:607
  340.4 17.0 %collective-permute-done.54.refs_2_.refs_1_ = bf16[768,256]{1,0:T(8,128)(2,1)S(1)} collective-permute-done((bf16[768,256]{1,0:T(8,128)(2,1)}, bf16[768,256]{1,0:T(8,128)(2,1)S(1)}, u32[]{:S(2)}, u32[]{:S(2)}) %collective-permute-start.54) | collective-permute-done | bytes 393248 | tf_op jit(solution)/shard_map/cond/branch_1_fun/ppermute | solution.py:659
  360.2 6.5 %far_values.19.refs_0_.refs_1_.refs_12_ = bf16[1024,256]{1,0:T(8,128)(2,1)} custom-call(s32[10,128]{1,0:T(8,128)S(1)} %get-tuple-element.75.lists.refs_0_, s32[24,128]{1,0:T(8,128)S(1)} %get-tuple-element.76.table, bf16[768,256]{1,0:T(8,128)(2,1)} %branch_1_fun.45.after, bf16[1024,3072]{1,0:T(8,128)(2,1)} %get-tuple-element.89.after.p, ...), custom_call_target="tpu_custom_call" | custom-call | tf_op jit(solution)/shard_map/cond/branch_1_fun/far_values/pallas_call | solution.py:607
  375.4 10.5 %collective-permute-done.55.refs_3_.refs_2_ = bf16[768,256]{1,0:T(8,128)(2,1)S(1)} collective-permute-done((bf16[768,256]{1,0:T(8,128)(2,1)}, bf16[768,256]{1,0:T(8,128)(2,1)S(1)}, u32[]{:S(2)}, u32[]{:S(2)}) %collective-permute-start.55) | collective-permute-done | bytes 393248 | tf_op jit(solution)/shard_map/cond/branch_1_fun/ppermute | solution.py:659
  391.8 7.1 %collective-permute-done.58.refs_3_.refs_6_ = bf16[768,256]{1,0:T(8,128)(2,1)S(1)} collective-permute-done((bf16[768,256]{1,0:T(8,128)(2,1)}, bf16[768,256]{1,0:T(8,128)(2,1)S(1)}, u32[]{:S(2)}, u32[]{:S(2)}) %collective-permute-start.58) | collective-permute-done | bytes 393248 | tf_op jit(solution)/shard_map/cond/branch_1_fun/ppermute | solution.py:659
  425.1 8.4 %collective-permute-done.65.refs_15_ = bf16[768,256]{1,0:T(8,128)(2,1)S(1)} collective-permute-done((bf16[768,256]{1,0:T(8,128)(2,1)}, bf16[768,256]{1,0:T(8,128)(2,1)S(1)}, u32[]{:S(2)}, u32[]{:S(2)}) %collective-permute-start.65) | collective-permute-done | bytes 393248 | tf_op jit(solution)/shard_map/cond/branch_1_fun/ppermute | solution.py:659
  433.6 7.4 %collective-permute-done.63.refs_11_ = bf16[768,256]{1,0:T(8,128)(2,1)S(1)} collective-permute-done((bf16[768,256]{1,0:T(8,128)(2,1)S(1)}, bf16[768,256]{1,0:T(8,128)(2,1)S(1)}, u32[]{:S(2)}, u32[]{:S(2)}) %collective-permute-start.63) | collective-permute-done | bytes 393248 | tf_op jit(solution)/shard_map/cond/branch_1_fun/ppermute | solution.py:659
  (175 shorter events, 190.3 us)
Async XLA Ops:
  25.2 36.1 %collective-permute-start.34 = (bf16[2944,128]{1,0:T(8,128)(2,1)}, bf16[2944,128]{1,0:T(8,128)(2,1)S(1)}, u32[]{:S(2)}, u32[]{:S(2)}) collective-permute-start(bf16[2944,128]{1,0:T(8,128)(2,1)} %branch_1_fun.27.after), channel_id=1, source_target_pairs={{0,16},{4,20},{8,24},{12,28},{16,0},{20,4},{24,8},{28,12},{1,17},{... | collective-permute-start | bytes 2261000 | tf_op jit(solution)/shard_map/cond/branch_1_fun/ppermute | solution.py:659
  66.4 67.1 %collective-permute-start.37 = (bf16[3712,128]{1,0:T(8,128)(2,1)}, bf16[3712,128]{1,0:T(8,128)(2,1)}, u32[]{:S(2)}, u32[]{:S(2)}) collective-permute-start(bf16[3712,128]{1,0:T(8,128)(2,1)} %branch_1_fun.29.refs_0_), channel_id=1, source_target_pairs={{0,8},{4,12},{8,0},{12,4},{16,24},{20,28},{24,16},{28,20},{1,9},{5... | collective-permute-start | bytes 2850824 | tf_op jit(solution)/shard_map/cond/branch_1_fun/ppermute | solution.py:659
  66.5 50.4 %collective-permute-start.36 = (bf16[2944,128]{1,0:T(8,128)(2,1)S(1)}, bf16[2944,128]{1,0:T(8,128)(2,1)}, u32[]{:S(2)}, u32[]{:S(2)}) collective-permute-start(bf16[2944,128]{1,0:T(8,128)(2,1)S(1)} %copy-done.21), channel_id=1, source_target_pairs={{0,16},{4,20},{8,24},{12,28},{16,0},{20,4},{24,8},{28,12},{1,17},{... | collective-permute-start | bytes 2261000 | tf_op jit(solution)/shard_map/cond/branch_1_fun/ppermute | solution.py:659
  67.7 47.2 %collective-permute-start.35 = (bf16[256,1024]{1,0:T(8,128)(2,1)S(1)}, bf16[256,1024]{1,0:T(8,128)(2,1)}, u32[]{:S(2)}, u32[]{:S(2)}) collective-permute-start(bf16[256,1024]{1,0:T(8,128)(2,1)S(1)} %copy-done.32), channel_id=1, source_target_pairs={{0,16},{4,20},{1,17},{5,21},{2,18},{6,22},{3,19},{7,23}} | collective-permute-start | bytes 1572872 | tf_op jit(solution)/shard_map/cond/branch_1_fun/ppermute | solution.py:659
  116.9 40.3 %collective-permute-start.41 = (bf16[2208,128]{1,0:T(8,128)(2,1)}, bf16[2208,128]{1,0:T(8,128)(2,1)}, u32[]{:S(2)}, u32[]{:S(2)}) collective-permute-start(bf16[2208,128]{1,0:T(8,128)(2,1)} %hold.21.refs_0_), channel_id=1, source_target_pairs={{0,16},{4,20},{8,24},{12,28},{16,0},{20,4},{24,8},{28,12},{1,17},{... | collective-permute-start | bytes 1695752 | tf_op jit(solution)/shard_map/cond/branch_1_fun/ppermute | solution.py:659
  120.4 24.7 %collective-permute-start.38 = (bf16[256,1024]{1,0:T(8,128)(2,1)}, bf16[256,1024]{1,0:T(8,128)(2,1)}, u32[]{:S(2)}, u32[]{:S(2)}) collective-permute-start(bf16[256,1024]{1,0:T(8,128)(2,1)} %either.21.after.a), channel_id=1, source_target_pairs={{0,8},{4,12},{16,24},{20,28},{1,9},{5,13},{17,25},{21,29},{2,10},{... | collective-permute-start | bytes 1572872 | tf_op jit(solution)/shard_map/cond/branch_1_fun/ppermute | solution.py:659
  125.5 30.9 %collective-permute-start.40 = (bf16[128,2048]{1,0:T(8,128)(2,1)}, bf16[128,2048]{1,0:T(8,128)(2,1)S(1)}, u32[]{:S(2)}, u32[]{:S(2)}) collective-permute-start(bf16[128,2048]{1,0:T(8,128)(2,1)} %get-tuple-element.80.refs_0_), channel_id=1, source_target_pairs={{0,4},{4,8},{8,12},{12,16},{16,20},{20,24},{24,28},{1,5},{5,9},{9,... | collective-permute-start | bytes 1572872 | tf_op jit(solution)/shard_map/cond/branch_1_fun/ppermute | solution.py:659
  133.5 43.3 %collective-permute-start.42 = (bf16[3712,128]{1,0:T(8,128)(2,1)}, bf16[3712,128]{1,0:T(8,128)(2,1)}, u32[]{:S(2)}, u32[]{:S(2)}) collective-permute-start(bf16[3712,128]{1,0:T(8,128)(2,1)} %branch_1_fun.31.refs_0_), channel_id=1, source_target_pairs={{0,8},{4,12},{8,0},{12,4},{16,24},{20,28},{24,16},{28,20},{1,9},{5... | collective-permute-start | bytes 2850824 | tf_op jit(solution)/shard_map/cond/branch_1_fun/ppermute | solution.py:659
  157.2 37.0 %collective-permute-start.44 = (bf16[2208,128]{1,0:T(8,128)(2,1)}, bf16[2208,128]{1,0:T(8,128)(2,1)S(1)}, u32[]{:S(2)}, u32[]{:S(2)}) collective-permute-start(bf16[2208,128]{1,0:T(8,128)(2,1)} %hold.23.refs_0_), channel_id=1, source_target_pairs={{0,16},{4,20},{8,24},{12,28},{16,0},{20,4},{24,8},{28,12},{1,17},{... | collective-permute-start | bytes 1695752 | tf_op jit(solution)/shard_map/cond/branch_1_fun/ppermute | solution.py:659
  157.2 24.7 %collective-permute-start.43 = (bf16[256,1024]{1,0:T(8,128)(2,1)}, bf16[256,1024]{1,0:T(8,128)(2,1)}, u32[]{:S(2)}, u32[]{:S(2)}) collective-permute-start(bf16[256,1024]{1,0:T(8,128)(2,1)} %either.22.after.a.b), channel_id=1, source_target_pairs={{0,4},{4,0},{8,12},{12,8},{16,20},{20,16},{24,28},{28,24},{1,5},{5... | collective-permute-start | bytes 1572872 | tf_op jit(solution)/shard_map/cond/branch_1_fun/ppermute | solution.py:659
  160.8 54.6 %collective-permute-start.45 = (bf16[2784,128]{1,0:T(8,128)(2,1)}, bf16[2784,128]{1,0:T(8,128)(2,1)S(1)}, u32[]{:S(2)}, u32[]{:S(2)}) collective-permute-start(bf16[2784,128]{1,0:T(8,128)(2,1)} %branch_1_fun.34.refs_0_), channel_id=1, source_target_pairs={{0,8},{4,12},{8,0},{12,4},{16,24},{20,28},{24,16},{28,20},{1,9},{5... | collective-permute-start | bytes 2138120 | tf_op jit(solution)/shard_map/cond/branch_1_fun/ppermute | solution.py:659
  198.6 42.5 %collective-permute-start.47 = (bf16[2784,128]{1,0:T(8,128)(2,1)}, bf16[2784,128]{1,0:T(8,128)(2,1)}, u32[]{:S(2)}, u32[]{:S(2)}) collective-permute-start(bf16[2784,128]{1,0:T(8,128)(2,1)} %branch_1_fun.37.refs_0_), channel_id=1, source_target_pairs={{0,8},{4,12},{8,0},{12,4},{16,24},{20,28},{24,16},{28,20},{1,9},{5... | collective-permute-start | bytes 2138120 | tf_op jit(solution)/shard_map/cond/branch_1_fun/ppermute | solution.py:659
  203.9 24.9 %collective-permute-start.46 = (bf16[1472,128]{1,0:T(8,128)(2,1)}, bf16[1472,128]{1,0:T(8,128)(2,1)S(1)}, u32[]{:S(2)}, u32[]{:S(2)}) collective-permute-start(bf16[1472,128]{1,0:T(8,128)(2,1)} %hold.24.refs_0_), channel_id=1, source_target_pairs={{0,16},{4,20},{8,24},{12,28},{16,0},{20,4},{24,8},{28,12},{1,17},{... | collective-permute-start | bytes 1130504 | tf_op jit(solution)/shard_map/cond/branch_1_fun/ppermute | solution.py:659
  213.4 42.4 %collective-permute-start.49 = (bf16[4352,128]{1,0:T(8,128)(2,1)}, bf16[4352,128]{1,0:T(8,128)(2,1)}, u32[]{:S(2)}, u32[]{:S(2)}) collective-permute-start(bf16[4352,128]{1,0:T(8,128)(2,1)} %branch_1_fun.33.after), channel_id=1, source_target_pairs={{0,4},{4,0},{8,12},{12,8},{16,20},{20,16},{24,28},{28,24},{1,5},{5... | collective-permute-start | bytes 3342344 | tf_op jit(solution)/shard_map/cond/branch_1_fun/ppermute | solution.py:659
  213.4 51.6 %collective-permute-start.50 = (bf16[4352,128]{1,0:T(8,128)(2,1)}, bf16[4352,128]{1,0:T(8,128)(2,1)}, u32[]{:S(2)}, u32[]{:S(2)}) collective-permute-start(bf16[4352,128]{1,0:T(8,128)(2,1)} %branch_1_fun.36.after), channel_id=1, source_target_pairs={{0,4},{4,0},{8,12},{12,8},{16,20},{20,16},{24,28},{28,24},{1,5},{5... | collective-permute-start | bytes 3342344 | tf_op jit(solution)/shard_map/cond/branch_1_fun/ppermute | solution.py:659
  241.1 41.8 %collective-permute-start.51 = (bf16[3264,128]{1,0:T(8,128)(2,1)}, bf16[3264,128]{1,0:T(8,128)(2,1)S(1)}, u32[]{:S(2)}, u32[]{:S(2)}) collective-permute-start(bf16[3264,128]{1,0:T(8,128)(2,1)} %branch_1_fun.38.after), channel_id=1, source_target_pairs={{0,4},{4,0},{8,12},{12,8},{16,20},{20,16},{24,28},{28,24},{1,5},{5... | collective-permute-start | bytes 2506760 | tf_op jit(solution)/shard_map/cond/branch_1_fun/ppermute | solution.py:659
  245.4 64.9 %collective-permute-start.52 = (bf16[3264,128]{1,0:T(8,128)(2,1)}, bf16[3264,128]{1,0:T(8,128)(2,1)}, u32[]{:S(2)}, u32[]{:S(2)}) collective-permute-start(bf16[3264,128]{1,0:T(8,128)(2,1)} %branch_1_fun.40.refs_0_), channel_id=1, source_target_pairs={{0,4},{4,0},{8,12},{12,8},{16,20},{20,16},{24,28},{28,24},{1,5},{5... | collective-permute-start | bytes 2506760 | tf_op jit(solution)/shard_map/cond/branch_1_fun/ppermute | solution.py:659
  255.8 54.6 %collective-permute-start.53 = (bf16[2176,128]{1,0:T(8,128)(2,1)}, bf16[2176,128]{1,0:T(8,128)(2,1)S(1)}, u32[]{:S(2)}, u32[]{:S(2)}) collective-permute-start(bf16[2176,128]{1,0:T(8,128)(2,1)} %branch_1_fun.41.after), channel_id=1, source_target_pairs={{0,4},{4,0},{8,12},{12,8},{16,20},{20,16},{24,28},{28,24},{1,5},{5... | collective-permute-start | bytes 1671176 | tf_op jit(solution)/shard_map/cond/branch_1_fun/ppermute | solution.py:659
  319.6 37.8 %collective-permute-start.54 = (bf16[768,256]{1,0:T(8,128)(2,1)}, bf16[768,256]{1,0:T(8,128)(2,1)S(1)}, u32[]{:S(2)}, u32[]{:S(2)}) collective-permute-start(bf16[768,256]{1,0:T(8,128)(2,1)} %branch_1_fun.42.after), channel_id=1, source_target_pairs={{16,0},{20,4},{24,8},{28,12},{17,1},{21,5},{25,9},{29,13},{18,2},{... | collective-permute-start | bytes 1179656 | tf_op jit(solution)/shard_map/cond/branch_1_fun/ppermute | solution.py:659
  329.4 39.3 %collective-permute-start.56 = (bf16[768,256]{1,0:T(8,128)(2,1)}, bf16[768,256]{1,0:T(8,128)(2,1)S(1)}, u32[]{:S(2)}, u32[]{:S(2)}) collective-permute-start(bf16[768,256]{1,0:T(8,128)(2,1)} %branch_1_fun.43.after), channel_id=1, source_target_pairs={{16,0},{20,4},{24,8},{28,12},{17,1},{21,5},{25,9},{29,13},{18,2},{... | collective-permute-start | bytes 1179656 | tf_op jit(solution)/shard_map/cond/branch_1_fun/ppermute | solution.py:659
  339.1 49.8 %collective-permute-start.59 = (bf16[768,256]{1,0:T(8,128)(2,1)}, bf16[768,256]{1,0:T(8,128)(2,1)S(1)}, u32[]{:S(2)}, u32[]{:S(2)}) collective-permute-start(bf16[768,256]{1,0:T(8,128)(2,1)} %branch_1_fun.44.refs_0_), channel_id=1, source_target_pairs={{16,0},{20,4},{24,8},{28,12},{17,1},{21,5},{25,9},{29,13},{18,2},{... | collective-permute-start | bytes 1179656 | tf_op jit(solution)/shard_map/cond/branch_1_fun/ppermute | solution.py:659
  360.2 25.7 %collective-permute-start.55 = (bf16[768,256]{1,0:T(8,128)(2,1)}, bf16[768,256]{1,0:T(8,128)(2,1)S(1)}, u32[]{:S(2)}, u32[]{:S(2)}) collective-permute-start(bf16[768,256]{1,0:T(8,128)(2,1)} %branch_1_fun.45.after), channel_id=1, source_target_pairs={{0,8},{4,12},{8,0},{12,4},{16,24},{20,28},{24,16},{28,20},{1,9},{5... | collective-permute-start | bytes 1179656 | tf_op jit(solution)/shard_map/cond/branch_1_fun/ppermute | solution.py:659
  371.5 27.4 %collective-permute-start.58 = (bf16[768,256]{1,0:T(8,128)(2,1)}, bf16[768,256]{1,0:T(8,128)(2,1)S(1)}, u32[]{:S(2)}, u32[]{:S(2)}) collective-permute-start(bf16[768,256]{1,0:T(8,128)(2,1)} %branch_1_fun.47.refs_0_), channel_id=1, source_target_pairs={{0,8},{4,12},{8,0},{12,4},{16,24},{20,28},{24,16},{28,20},{1,9},{5... | collective-permute-start | bytes 1179656 | tf_op jit(solution)/shard_map/cond/branch_1_fun/ppermute | solution.py:659
  374.1 27.8 %collective-permute-start.62 = (bf16[768,256]{1,0:T(8,128)(2,1)S(1)}, bf16[768,256]{1,0:T(8,128)(2,1)S(1)}, u32[]{:S(2)}, u32[]{:S(2)}) collective-permute-start(bf16[768,256]{1,0:T(8,128)(2,1)S(1)} %copy-done.62), channel_id=1, source_target_pairs={{16,0},{20,4},{24,8},{28,12},{17,1},{21,5},{25,9},{29,13},{18,2},{... | collective-permute-start | bytes 1179656 | tf_op jit(solution)/shard_map/cond/branch_1_fun/ppermute | solution.py:659
  (41 other events, 317.0 us)
